TPU v7x, 256 devices: a 4x2x16 block of a 4x16x16 slice. The times are simulated.
256 devices in a mesh: groups: 2 (over y), ctx: 16 (over z), head: 4 (over x), pair: 2 (over core).
Axes of the slice: x: 4, y: 2, z: 16, core: 2. Of those that a mesh axis runs over, the one named last changes fastest.
The devices are a block of a 4x16x16 slice.
Arguments:
- queries: bfloat16 [512, 32, 128], P('groups', 'head'), parts along dimension 0, may hold values from -80 to 80
- prompt_keys: bfloat16 [131072, 4, 128], P(('groups', 'ctx', 'pair'), 'head'), parts along dimension 0, may hold values from -32 to 32
- prompt_values: bfloat16 [131072, 4, 128], P(('groups', 'ctx', 'pair'), 'head'), parts along dimension 0, may hold values from -6 to 6
- residual: bfloat16 [512, 2048], P(('groups', 'ctx', 'head', 'pair')), parts along dimension 0, may hold values from -0.59765625 to 0.59765625
- out_weight: bfloat16 [4096, 2048], P('head', 'ctx'), may hold values from -0.09375 to 0.09375
- norm_gain: float32 [2048], replicated, may hold values from 0.1 to 1.9
- expert_lists: int32 [512, 8], P(('groups', 'ctx')), parts along dimension 0, may hold values from 0 to 127, all different within a row; in each aligned block of 16 rows (0 to 15, 16 to 31, ...) at most 2 rows name the same one
- gate_weights: float32 [512, 8], P(('groups', 'ctx')), parts along dimension 0, may hold values from 0.05 to 0.4
- gate_up: bfloat16 [128, 2048, 1536], P(('ctx', 'head', 'pair')), may hold values from -0.125 to 0.125
- down_proj: bfloat16 [128, 768, 2048], P(('ctx', 'head', 'pair')), may hold values from -0.21875 to 0.21875
Outputs:
- layer_out: bfloat16 [512, 2048], P(('groups', 'ctx', 'head', 'pair')), parts along dimension 0
There are 2 independent parts, one for each index of `groups`. A program takes and returns all parts, laid end to end along the dimension named above; an argument that names none is the same for every part. Nothing has to cross between parts.
Inputs may be any that keep to these rules, and one draw needn't show every extreme that they name: `expert_lists`: A row names 8 different experts. In each aligned block of 16 rows (the rows of one index of ctx) no expert is named by more than 2 rows.
All inputs are finite; a program needn't handle non-finite values.
Results may differ from a plain program's by a relative error of at most 0.018.
Values may be sent and summed in bfloat16 or wider, within the bound.
No kernel may reach another device: no remote copies, remote signals or barrier semaphores. Data moves between devices by JAX's collectives and lax.ppermute only.
A program may use at most 128 MiB of HBM per device.

v0:
```python
import math

import jax
import jax.numpy as jnp
from jax import lax
from jax.sharding import PartitionSpec as P


def cut_along(shard, dim, devices):
    shape = shard.shape
    parts = shard.reshape(*shape[:dim], devices, shape[dim] // devices, *shape[dim + 1 :])
    return jnp.moveaxis(parts, dim, 0)


def laid_out(parts, dim):
    parts = jnp.moveaxis(parts, 0, dim)
    shape = parts.shape
    return parts.reshape(*shape[:dim], shape[dim] * shape[dim + 1], *shape[dim + 2 :])


def one_exchange(shard, axis, axes, splits, concats):
    sizes = [lax.axis_size(a) for a in axes]
    parts = cut_along(shard, splits[0], sizes[0])
    parts = jnp.moveaxis(cut_along(parts, splits[1] + 1, sizes[1]), 0, 1)
    inside = parts.shape[2:]
    parts = parts.reshape(-1, *inside)
    parts = lax.all_to_all(parts, axis, split_axis=0, concat_axis=0, tiled=True)
    parts = laid_out(parts.reshape(*sizes, *inside), concats[0] + 1)
    return laid_out(parts, concats[1])


def sum_at_owner(shard, axis, dim):
    devices = lax.axis_size(axis)
    parts = lax.all_to_all(cut_along(shard, dim, devices), axis, 0, 0, tiled=True)
    return jnp.sum(parts, axis=0)


def local_partials(queries, prompt_keys, prompt_values):
    rows_all, heads_here, head_size = queries.shape
    length_here, kv_here, width_keys = prompt_keys.shape
    group = heads_here // kv_here
    block = min(1024, length_here)
    grouped = queries.reshape(rows_all, kv_here, group, head_size)
    key_blocks = prompt_keys.reshape(length_here // block, block, kv_here, head_size)
    value_blocks = prompt_values.reshape(length_here // block, block, kv_here, head_size)
    scale_factor = 1.0 / math.sqrt(head_size)

    def step(carry, pieces):
        running, total, numer = carry
        key_piece, value_piece = pieces
        scores = (
            jnp.einsum("rkgd,tkd->rkgt", grouped, key_piece, preferred_element_type=jnp.float32)
            * scale_factor
        )
        fresh = jnp.maximum(running, jnp.max(scores, axis=3))
        decay = jnp.exp(running - fresh)
        weights = jnp.exp(scores - fresh[..., None])
        total = total * decay + jnp.sum(weights, axis=3)
        numer = numer * decay[..., None] + jnp.einsum(
            "rkgt,tkd->rkgd",
            weights.astype(jnp.bfloat16),
            value_piece,
            preferred_element_type=jnp.float32,
        )
        return ((fresh, total, numer), None)

    stats_shape = (rows_all, kv_here, group)
    start = (
        jnp.full(stats_shape, -jnp.inf, jnp.float32),
        jnp.zeros(stats_shape, jnp.float32),
        jnp.zeros(stats_shape + (head_size,), jnp.float32),
    )
    (running, total, numer), unused = lax.scan(step, start, (key_blocks, value_blocks))
    return (numer, running, total)


def run_experts(grouped, gate_up, down_proj):
    hidden_units = down_proj.shape[1]
    both = jnp.einsum("sjcd,jdf->sjcf", grouped, gate_up, preferred_element_type=jnp.float32)
    inner = (jax.nn.silu(both[..., :hidden_units]) * both[..., hidden_units:]).astype(jnp.bfloat16)
    return jnp.einsum(
        "sjcf,jfd->sjcd", inner, down_proj, preferred_element_type=jnp.float32
    ).astype(jnp.bfloat16)


def exclusive_rank(identities, n_experts):
    onehot = (identities[:, None] == jnp.arange(n_experts, dtype=jnp.int32)[None, :]).astype(
        jnp.int32
    )
    before = jnp.cumsum(onehot, axis=0) - onehot
    return jnp.sum(before * onehot, axis=1)


def body(
    queries,
    prompt_keys,
    prompt_values,
    residual,
    out_weight,
    norm_gain,
    expert_lists,
    gate_weights,
    gate_up,
    down_proj,
):
    n_ctx = lax.axis_size("ctx")
    n_head = lax.axis_size("head")
    n_pair = lax.axis_size("pair")
    rows_here, width = residual.shape
    numer, running, total = local_partials(queries, prompt_keys, prompt_values)
    split = (n_ctx, n_head, n_pair, rows_here)
    numer = numer.reshape(split + numer.shape[1:])
    running = running.reshape(split + running.shape[1:])
    total = total.reshape(split + total.shape[1:])
    numer, running, total = (
        one_exchange(numer, ("ctx", "pair"), ("ctx", "pair"), (0, 2), (0, 2)),
        one_exchange(running, ("ctx", "pair"), ("ctx", "pair"), (0, 2), (0, 2)),
        one_exchange(total, ("ctx", "pair"), ("ctx", "pair"), (0, 2), (0, 2)),
    )
    highest = jnp.max(running, axis=(0, 2), keepdims=True)
    scales = jnp.exp(running - highest)
    numer = jnp.sum(numer * scales[..., None], axis=(0, 2))
    total = jnp.sum(total * scales, axis=(0, 2))
    attended = (numer / total[..., None]).astype(jnp.bfloat16).reshape(n_head * rows_here, -1)
    partial_value = jnp.dot(
        attended,
        lax.all_gather(out_weight, "ctx", axis=1, tiled=True),
        preferred_element_type=jnp.float32,
    )
    projected = sum_at_owner(partial_value, "head", 0)
    hidden_state = (residual.astype(jnp.float32) + projected).astype(jnp.bfloat16)
    as_float = hidden_state.astype(jnp.float32)
    normed = (
        as_float
        * lax.rsqrt(jnp.mean(as_float * as_float, axis=1, keepdims=True) + 1e-06)
        * norm_gain
    ).astype(jnp.bfloat16)
    experts_here = gate_up.shape[0]
    n_experts = experts_here * n_ctx * n_head * n_pair
    block_rows_count, top = expert_lists.shape
    capacity = 2 * block_rows_count * top // n_experts
    owner = lax.axis_index("head") * n_pair + lax.axis_index("pair")
    block_rows = lax.all_gather(normed, ("head", "pair"), axis=0, tiled=True)
    identities = expert_lists.reshape(-1)
    slot_of = exclusive_rank(identities, n_experts)
    device_of = identities // experts_here
    local_of = identities % experts_here
    ctx_of = device_of // (n_head * n_pair)
    mine = device_of % (n_head * n_pair) == owner
    target = jnp.where(mine, (ctx_of * experts_here + local_of) * capacity + slot_of, -1)
    placing = (
        jnp.arange(n_ctx * experts_here * capacity, dtype=jnp.int32)[:, None] == target[None, :]
    ).astype(jnp.bfloat16)
    repeated = jnp.repeat(block_rows, top, axis=0)
    sending = jnp.dot(placing, repeated, preferred_element_type=jnp.float32).astype(jnp.bfloat16)
    sending = sending.reshape(n_ctx, experts_here, capacity, width)
    produced = run_experts(
        lax.all_to_all(sending, "ctx", split_axis=0, concat_axis=0, tiled=True), gate_up, down_proj
    )
    returned = lax.all_to_all(produced, "ctx", split_axis=0, concat_axis=0, tiled=True)
    picked = jnp.take(returned.reshape(-1, width), jnp.maximum(target, 0), axis=0)
    factor = jnp.where(mine, gate_weights.reshape(-1), jnp.zeros_like(gate_weights.reshape(-1)))
    partial_rows = jnp.sum(
        (picked.astype(jnp.float32) * factor[:, None]).reshape(block_rows_count, top, width), axis=1
    )
    mixture = sum_at_owner(partial_rows, ("head", "pair"), 0)
    return (hidden_state.astype(jnp.float32) + mixture).astype(jnp.bfloat16)


def solution(mesh):
    in_specs = (
        P("groups", "head", None),
        P(("groups", "ctx", "pair"), "head", None),
        P(("groups", "ctx", "pair"), "head", None),
        P(("groups", "ctx", "head", "pair"), None),
        P("head", "ctx"),
        P(),
        P(("groups", "ctx"), None),
        P(("groups", "ctx"), None),
        P(("ctx", "head", "pair"), None, None),
        P(("ctx", "head", "pair"), None, None),
    )
    out_specs = P(("groups", "ctx", "head", "pair"), None)
    return jax.shard_map(body, mesh=mesh, in_specs=in_specs, out_specs=out_specs, check_vma=False)
```

profile of v0, /device:TPU:33, one launch (start us, length us, event | category | flops | bytes accessed | tf_op | source)
XLA Modules:
  0.0 262.6 jit_solution(3554906184980611000)
XLA Ops:
  6.6 0.7 all-gather.3.cloned.1.call-update
  7.3 2.0 copy.138
  9.4 27.0 %while.15 = (s32[]{:T(128)}, f32[256,1,8]{0,2,1:T(8,128)S(1)}, f32[256,1,8]{0,2,1:T(8,128)S(1)}, f32[256,1,8,128]{0,3,2,1:T(8,128)}, bf16[2,1024,1,128]{3,1,2,0:...) while((s32[]{:T(128)}, f32[256,1,8]{0,2,1:T(8,128)S(1)}, ...), condition=%wide.region_3.4_spmd.clone, body=%wide.region_0.3_spmd.clone.sunk | while | flops 1091317760 | bytes 61998208 | solution.py:73
  9.4 5.6 %bitcast_reduce_fusion.3 = (f32[256,8]{0,1:T(8,128)S(1)}, f32[1024,256,8]{1,0,2:T(8,128)}) fusion(bf16[256,1,8,128]{3,0,2,1:T(8,128)(2,1)} %get-tuple-element.193, bf16[2,1024,1,128]{3,1,2,0:T(8,128)(2,1)} %get-tuple-element.192, s32[]{:T(128)} %get-tuple-element.179), kind=kOutput, calls=%fused_computation.2.clone.1 | convolution fusion | flops 541063168 | bytes 9183744 | tf_op jit(solution)/shard_map/while/body/eval_jaxpr/rkgd,tkd->rkgt/dot_general | solution.py:52
  15.0 6.4 %fusion.76 = f32[256,1,8,128]{0,3,2,1:T(8,128)} fusion(f32[1024,256,8]{1,0,2:T(8,128)} %get-tuple-element.168, f32[256,8]{0,1:T(8,128)S(1)} %bitcast.196, f32[256,1,8,128]{0,3,2,1:T(8,128)} %get-tuple-element.182, f32[256,8]{0,1:T(8,128)S(1)} %get-tuple-element.169, pred[]{:T(512)S(6)} %compare.45, ...), kind=kOutput, calls=%fused_computation.11.clone.1 | convolution fusion | flops 543948800 | bytes 10764801 | tf_op jit(solution)/shard_map/while/body/eval_jaxpr/rkgt,tkd->rkgd/dot_general | solution.py:59
  21.4 1.4 fusion.75
  22.8 5.6 %bitcast_reduce_fusion.3 = (f32[256,8]{0,1:T(8,128)S(1)}, f32[1024,256,8]{1,0,2:T(8,128)}) fusion(bf16[256,1,8,128]{3,0,2,1:T(8,128)(2,1)} %get-tuple-element.193, bf16[2,1024,1,128]{3,1,2,0:T(8,128)(2,1)} %get-tuple-element.192, s32[]{:T(128)} %get-tuple-element.179), kind=kOutput, calls=%fused_computation.2.clone.1 | convolution fusion | flops 541063168 | bytes 9183744 | tf_op jit(solution)/shard_map/while/body/eval_jaxpr/rkgd,tkd->rkgt/dot_general | solution.py:52
  28.4 6.6 %fusion.76 = f32[256,1,8,128]{0,3,2,1:T(8,128)} fusion(f32[1024,256,8]{1,0,2:T(8,128)} %get-tuple-element.168, f32[256,8]{0,1:T(8,128)S(1)} %bitcast.196, f32[256,1,8,128]{0,3,2,1:T(8,128)} %get-tuple-element.182, f32[256,8]{0,1:T(8,128)S(1)} %get-tuple-element.169, pred[]{:T(512)S(6)} %compare.45, ...), kind=kOutput, calls=%fused_computation.11.clone.1 | convolution fusion | flops 543948800 | bytes 10764801 | tf_op jit(solution)/shard_map/while/body/eval_jaxpr/rkgt,tkd->rkgd/dot_general | solution.py:59
  35.0 1.4 fusion.75
  36.4 0.1 copy.100
  36.5 0.1 copy.101
  36.6 0.7 copy.102
  37.3 25.6 %all-to-all-start.1 = ((f32[32,1,4,1,2,1,8]{6,4,2,5,3,1,0:T(2,128)}), f32[32,1,4,1,2,1,8]{6,4,2,5,3,1,0:T(2,128)S(1)}, u32[]{:S(2)}, u32[]{:S(2)}) async-start(f32[32,1,4,1,2,1,8]{6,4,2,5,3,1,0:T(2,128)} %copy.102), calls=%async_computation.1 | async-start | bytes 262144 | tf_op jit(solution)/shard_map/all_to_all | solution.py:27
  62.9 0.1 copy.105
  63.0 0.1 copy.106
  63.1 0.8 copy.107
  63.9 16.5 %all-to-all-done.1 = f32[32,1,4,1,2,1,8]{6,4,2,5,3,1,0:T(2,128)S(1)} async-done(((f32[32,1,4,1,2,1,8]{6,4,2,5,3,1,0:T(2,128)}), f32[32,1,4,1,2,1,8]{6,4,2,5,3,1,0:T(2,128)S(1)}, u32[]{:S(2)}, u32[]{:S(2)}) %all-to-all-start.1) | async-done | bytes 8224 | tf_op jit(solution)/shard_map/all_to_all | solution.py:27
  80.4 4.8 %all-to-all-start.2 = ((f32[32,1,4,1,2,1,8]{6,4,2,5,3,1,0:T(2,128)}), f32[32,1,4,1,2,1,8]{6,4,2,5,3,1,0:T(2,128)S(1)}, u32[]{:S(2)}, u32[]{:S(2)}) async-start(f32[32,1,4,1,2,1,8]{6,4,2,5,3,1,0:T(2,128)} %copy.107), calls=%async_computation.2 | async-start | bytes 262144 | tf_op jit(solution)/shard_map/all_to_all | solution.py:27
  85.2 2.6 copy.97
  87.8 2.4 copy.98
  90.1 12.6 %all-to-all-done.2 = f32[32,1,4,1,2,1,8]{6,4,2,5,3,1,0:T(2,128)S(1)} async-done(((f32[32,1,4,1,2,1,8]{6,4,2,5,3,1,0:T(2,128)}), f32[32,1,4,1,2,1,8]{6,4,2,5,3,1,0:T(2,128)S(1)}, u32[]{:S(2)}, u32[]{:S(2)}) %all-to-all-start.2) | async-done | bytes 8224 | tf_op jit(solution)/shard_map/all_to_all | solution.py:27
  102.7 5.6 %all-to-all-start = ((f32[32,1,4,1,2,1,8,128]{7,6,4,2,5,3,1,0:T(8,128)}), f32[32,1,4,1,2,1,8,128]{7,6,4,2,5,3,1,0:T(8,128)}, u32[]{:S(2)}, u32[]{:S(2)}) async-start(f32[32,1,4,1,2,1,8,128]{7,6,4,2,5,3,1,0:T(8,128)} %bitcast.198), calls=%async_computation | async-start | bytes 2097152 | tf_op jit(solution)/shard_map/all_to_all | solution.py:27
  108.4 0.1 copy.111
  108.4 0.1 reshape.404
  108.5 0.1 fusion.48
  108.6 0.2 reduce_window_sum.11
  108.8 0.7 select_reduce_fusion
  109.5 0.1 bitcast_reduce_fusion.1
  109.6 0.1 fusion.43
  109.7 0.1 copy.104
  109.8 0.2 fusion.46
  109.9 55.4 %all-to-all-done = f32[32,1,4,1,2,1,8,128]{7,6,4,2,5,3,1,0:T(8,128)} async-done(((f32[32,1,4,1,2,1,8,128]{7,6,4,2,5,3,1,0:T(8,128)}), f32[32,1,4,1,2,1,8,128]{7,6,4,2,5,3,1,0:T(8,128)}, u32[]{:S(2)}, u32[]{:S(2)}) %all-to-all-start) | async-done | bytes 1048608 | tf_op jit(solution)/shard_map/all_to_all | solution.py:27
  165.4 1.6 multiply_reduce_fusion.1
  166.9 0.1 divide_convert_fusion
  167.0 0.0 copy-start.2
  167.0 0.0 copy-start.4
  167.1 0.0 all-gather.3.cloned.1.call-done
  167.1 3.5 %fusion.26 = f32[4,2,2048]{2,1,0:T(2,128)} fusion(bf16[4,2,1024]{2,1,0:T(2,128)(2,1)S(1)} %convert_element_type.57, bf16[1024,2048]{1,0:T(8,128)(2,1)} %all-gather.3.cloned.1.call-done), kind=kOutput, calls=%fused_computation.29 | convolution fusion | flops 33554432 | bytes 4276224 | tf_op jit(solution)/shard_map/dot_general | solution.py:125
  170.6 6.1 %all-to-all-start.3 = ((f32[4,2,2048]{2,1,0:T(2,128)}), f32[4,2,2048]{2,1,0:T(2,128)S(1)}, u32[]{:S(2)}, u32[]{:S(2)}) async-start(f32[4,2,2048]{2,1,0:T(2,128)} %fusion.26), calls=%async_computation.3 | async-start | bytes 131072 | tf_op jit(solution)/shard_map/all_to_all | solution.py:34
  176.7 0.7 compare_select_fusion.1
  177.4 3.8 %all-to-all-done.3 = f32[4,2,2048]{2,1,0:T(2,128)S(1)} async-done(((f32[4,2,2048]{2,1,0:T(2,128)}), f32[4,2,2048]{2,1,0:T(2,128)S(1)}, u32[]{:S(2)}, u32[]{:S(2)}) %all-to-all-start.3) | async-done | bytes 65568 | tf_op jit(solution)/shard_map/all_to_all | solution.py:34
  181.2 0.8 fusion.51
  182.1 0.8 fusion.62
  182.8 14.6 %all-gather = bf16[8,2,2048]{2,1,0:T(2,128)(2,1)S(1)} all-gather(bf16[1,2,2048]{2,1,0:T(2,128)(2,1)S(1)} %fusion.62), channel_id=1, replica_groups=mesh['groups'=2,'ctx'=16,'head'=4,'pair'=2] {'head','pair'}, dimensions={0}, use_global_device_ids=true | all-gather | bytes 73728 | tf_op jit(solution)/shard_map/all_gather | solution.py:143
  197.5 0.2 convolution_convert_fusion
  197.7 0.8 reshape.406
  198.5 5.5 %all-to-all-start.4 = ((bf16[16,1,2,2048]{3,2,1,0:T(2,128)(2,1)}), bf16[16,1,2,2048]{3,2,1,0:T(2,128)(2,1)S(1)}, u32[]{:S(2)}, u32[]{:S(2)}) async-start(bf16[16,1,2,2048]{3,2,1,0:T(2,128)(2,1)} %bitcast.34), calls=%async_computation.4 | async-start | bytes 262144 | tf_op jit(solution)/shard_map/all_to_all | solution.py:158
  203.9 0.1 reshape.412
  204.0 0.7 maximum_bitcast_fusion
  204.7 11.1 %all-to-all-done.4 = bf16[16,1,2,2048]{3,2,1,0:T(2,128)(2,1)S(1)} async-done(((bf16[16,1,2,2048]{3,2,1,0:T(2,128)(2,1)}), bf16[16,1,2,2048]{3,2,1,0:T(2,128)(2,1)S(1)}, u32[]{:S(2)}, u32[]{:S(2)}) %all-to-all-start.4) | async-done | bytes 131104 | tf_op jit(solution)/shard_map/all_to_all | solution.py:158
  215.9 3.9 %fusion.30 = f32[16,1,2,1536]{3,0,2,1:T(8,128)S(1)} fusion(bf16[1,2048,1536]{2,1,0:T(8,128)(2,1)} %param.20, bf16[16,1,2,2048]{3,2,1,0:T(2,128)(2,1)S(1)} %all-to-all-done.4), kind=kOutput, calls=%fused_computation.33 | convolution fusion | flops 201326592 | bytes 6619136 | tf_op jit(solution)/shard_map/sjcd,jdf->sjcf/dot_general | solution.py:79
  219.8 0.6 fusion.36
  220.4 0.8 copy.118
  221.2 6.7 %all-to-all-start.5 = ((bf16[16,1,2,2048]{3,2,1,0:T(2,128)(2,1)}), bf16[16,1,2,2048]{3,2,1,0:T(2,128)(2,1)S(1)}, u32[]{:S(2)}, u32[]{:S(2)}) async-start(bf16[16,1,2,2048]{3,2,1,0:T(2,128)(2,1)} %copy.118), calls=%async_computation.5 | async-start | bytes 262144 | tf_op jit(solution)/shard_map/all_to_all | solution.py:160
  228.0 0.1 reduce_sum.82
  228.1 0.0 copy-done.4
  228.1 0.1 copy.120
  228.2 11.6 %all-to-all-done.5 = bf16[16,1,2,2048]{3,2,1,0:T(2,128)(2,1)S(1)} async-done(((bf16[16,1,2,2048]{3,2,1,0:T(2,128)(2,1)}), bf16[16,1,2,2048]{3,2,1,0:T(2,128)(2,1)S(1)}, u32[]{:S(2)}, u32[]{:S(2)}) %all-to-all-start.5) | async-done | bytes 131104 | tf_op jit(solution)/shard_map/all_to_all | solution.py:160
  239.7 0.1 reshape.411
  239.8 1.7 gather_fusion
  241.5 2.0 multiply_reduce_fusion
  243.5 0.1 reshape.413
  243.6 11.5 %all_to_all.35 = f32[8,2,2048]{2,1,0:T(2,128)S(1)} all-to-all(f32[8,2,2048]{2,1,0:T(2,128)S(1)} %reshape.413), channel_id=1, replica_groups=mesh['groups'=2,'ctx'=16,'head'=4,'pair'=2] {'head','pair'}, dimensions={0} | all-to-all | bytes 262144 | tf_op jit(solution)/shard_map/all_to_all | solution.py:34
  255.1 0.6 fusion.54
  (27 shorter events, 0.2 us)
Async XLA Ops:
  6.5 213.3 %copy-start = (bf16[1,768,2048]{2,1,0:T(8,128)(2,1)S(1)}, bf16[1,768,2048]{2,1,0:T(8,128)(2,1)}, u32[]{:S(2)}) copy-start(bf16[1,768,2048]{2,1,0:T(8,128)(2,1)} %param.21) | copy-start | bytes 9437188
  6.6 160.5 %all-gather.3.cloned.1.call-start = ((), (), s32[]{:S(2)}) async-start(), calls=%async_computation.7 | async-start | bytes 4456448 | tf_op jit(solution)/shard_map/all_gather | solution.py:127
  9.4 99.0 %copy-start.3 = (s32[16,8]{0,1:T(8,128)S(1)}, s32[16,8]{0,1:T(8,128)}, u32[]{:S(2)}) copy-start(s32[16,8]{0,1:T(8,128)} %param.18) | copy-start | bytes 1540
  15.0 6.4 %copy-start.1 = (f32[1024,256,8]{1,0,2:T(8,128)S(1)}, f32[1024,256,8]{1,0,2:T(8,128)}, u32[]{:S(2)}) copy-start(f32[1024,256,8]{1,0,2:T(8,128)} %get-tuple-element.168) | copy-start | bytes 25165828 | tf_op jit(solution)/shard_map/while
  28.4 6.6 %copy-start.1 = (f32[1024,256,8]{1,0,2:T(8,128)S(1)}, f32[1024,256,8]{1,0,2:T(8,128)}, u32[]{:S(2)}) copy-start(f32[1024,256,8]{1,0,2:T(8,128)} %get-tuple-element.168) | copy-start | bytes 25165828 | tf_op jit(solution)/shard_map/while
  37.3 43.0 %all-to-all-start.1 = ((f32[32,1,4,1,2,1,8]{6,4,2,5,3,1,0:T(2,128)}), f32[32,1,4,1,2,1,8]{6,4,2,5,3,1,0:T(2,128)S(1)}, u32[]{:S(2)}, u32[]{:S(2)}) async-start(f32[32,1,4,1,2,1,8]{6,4,2,5,3,1,0:T(2,128)} %copy.102), calls=%async_computation.1 | async-start | bytes 262144 | tf_op jit(solution)/shard_map/all_to_all | solution.py:27
  80.4 22.3 %all-to-all-start.2 = ((f32[32,1,4,1,2,1,8]{6,4,2,5,3,1,0:T(2,128)}), f32[32,1,4,1,2,1,8]{6,4,2,5,3,1,0:T(2,128)S(1)}, u32[]{:S(2)}, u32[]{:S(2)}) async-start(f32[32,1,4,1,2,1,8]{6,4,2,5,3,1,0:T(2,128)} %copy.107), calls=%async_computation.2 | async-start | bytes 262144 | tf_op jit(solution)/shard_map/all_to_all | solution.py:27
  102.7 62.7 %all-to-all-start = ((f32[32,1,4,1,2,1,8,128]{7,6,4,2,5,3,1,0:T(8,128)}), f32[32,1,4,1,2,1,8,128]{7,6,4,2,5,3,1,0:T(8,128)}, u32[]{:S(2)}, u32[]{:S(2)}) async-start(f32[32,1,4,1,2,1,8,128]{7,6,4,2,5,3,1,0:T(8,128)} %bitcast.198), calls=%async_computation | async-start | bytes 2097152 | tf_op jit(solution)/shard_map/all_to_all | solution.py:27
  167.0 60.9 %copy-start.2 = (s32[128]{0:T(128)S(1)}, s32[128]{0:T(128)}, u32[]{:S(2)}) copy-start(s32[128]{0:T(128)} %select_reduce_fusion) | copy-start | bytes 1540
  167.0 61.0 %copy-start.4 = (f32[16,8]{0,1:T(8,128)S(1)}, f32[16,8]{0,1:T(8,128)}, u32[]{:S(2)}) copy-start(f32[16,8]{0,1:T(8,128)} %param.19) | copy-start | bytes 1540
  170.6 10.6 %all-to-all-start.3 = ((f32[4,2,2048]{2,1,0:T(2,128)}), f32[4,2,2048]{2,1,0:T(2,128)S(1)}, u32[]{:S(2)}, u32[]{:S(2)}) async-start(f32[4,2,2048]{2,1,0:T(2,128)} %fusion.26), calls=%async_computation.3 | async-start | bytes 131072 | tf_op jit(solution)/shard_map/all_to_all | solution.py:34
  198.5 17.4 %all-to-all-start.4 = ((bf16[16,1,2,2048]{3,2,1,0:T(2,128)(2,1)}), bf16[16,1,2,2048]{3,2,1,0:T(2,128)(2,1)S(1)}, u32[]{:S(2)}, u32[]{:S(2)}) async-start(bf16[16,1,2,2048]{3,2,1,0:T(2,128)(2,1)} %bitcast.34), calls=%async_computation.4 | async-start | bytes 262144 | tf_op jit(solution)/shard_map/all_to_all | solution.py:158
  221.2 18.5 %all-to-all-start.5 = ((bf16[16,1,2,2048]{3,2,1,0:T(2,128)(2,1)}), bf16[16,1,2,2048]{3,2,1,0:T(2,128)(2,1)S(1)}, u32[]{:S(2)}, u32[]{:S(2)}) async-start(bf16[16,1,2,2048]{3,2,1,0:T(2,128)(2,1)} %copy.118), calls=%async_computation.5 | async-start | bytes 262144 | tf_op jit(solution)/shard_map/all_to_all | solution.py:160
Sparse Core Ops, SparseCore 0:
  9.1 119.6 all-gather.2
where the time goes:
time: 264 us; the launch traced here: 263 us
  waiting for transfers between devices  112 us (42%)
  starting transfers between devices  54.3 us (21%)
  matrix products  32.4 us (12%)
  blocking collectives  26.1 us (10%)
  between operations  13.7 us (5%)
  local copies, waits for them, and re-layouts  12.9 us (5%)
  other arithmetic  11.4 us (4%)
    all_to_all x3, waiting for transfers between devices, one_exchange(): parts = lax.all_to_all(parts, axis, split_axis=0, concat_axis=0, tiled=True)  84.5 us
    all_to_all x3, starting transfers between devices, one_exchange(): parts = lax.all_to_all(parts, axis, split_axis=0, concat_axis=0, tiled=True)  36 us
    all_gather x1, blocking collectives, body(): block_rows = lax.all_gather(normed, ('head', 'pair'), axis=0, tiled=True)  14.6 us
    dot_general x2, matrix products, step(): jnp.einsum('rkgt,tkd->rkgd', weights.astype(jnp.bfloat16), value_piece, p...  12.9 us
    all_to_all x1, waiting for transfers between devices, body(): lax.all_to_all(produced, 'ctx', split_axis=0, concat_axis=0, tiled=True)  11.6 us
    all_to_all x1, blocking collectives, sum_at_owner(): lax.all_to_all(cut_along(shard, dim, devices), axis, 0, 0, tiled=True)  11.5 us
    dot_general x2, matrix products, step(): jnp.einsum('rkgd,tkd->rkgt', grouped, key_piece, preferred_element_type=j...  11.2 us
    all_to_all x1, waiting for transfers between devices, body(): lax.all_to_all(sending, 'ctx', split_axis=0, concat_axis=0, tiled=True)  11.1 us
  transfers between devices with their start and end apart: 7, of which 6 were waited for; matrix products, arithmetic and copies ran while one was open for 15% of the time, Pallas kernels for 0%

commit v1 on v0

v1 whole, which is shorter than its diff:
```python
import math

import jax
import jax.numpy as jnp
from jax import lax
from jax.experimental import pallas as pl
from jax.experimental.pallas import tpu as pltpu
from jax.sharding import PartitionSpec as P

F32 = jnp.float32
BF16 = jnp.bfloat16
STATS = 8


def iota(shape, dim):
    return lax.broadcasted_iota(jnp.int32, shape, dim)


def dot(a, b):
    return lax.dot_general(a, b, (((1,), (0,)), ((), ())), preferred_element_type=F32)


def as_row(column, lanes):
    n = column.shape[0]
    here = iota((n, lanes), 0) == iota((n, lanes), 1)
    return jnp.sum(jnp.where(here, jnp.broadcast_to(column, (n, lanes)), 0.0), axis=0, keepdims=True)


def as_column(row, n):
    lanes = row.shape[1]
    here = iota((n, lanes), 0) == iota((n, lanes), 1)
    return jnp.sum(jnp.where(here, jnp.broadcast_to(row, (n, lanes)), 0.0), axis=1, keepdims=True)


def pieces(row):
    first = row.astype(BF16).astype(F32)
    second = (row - first).astype(BF16).astype(F32)
    third = row - first - second
    return first, second, third


def stacked(rows, lanes):
    at = iota((STATS, lanes), 0)
    out = jnp.zeros((STATS, lanes), F32)
    for i, row in enumerate(rows):
        out = jnp.where(at == i, jnp.broadcast_to(row, (STATS, lanes)), out)
    return out


def attend_half(half, queries, keys, values, blocks, pairs_block):
    units, _, unit, width = queries.shape
    length = keys.shape[0]
    tile_blocks = max(1, 256 // pairs_block)
    steps = blocks // tile_blocks
    tile_units = units // steps
    tile = tile_units * unit
    scale = 1.0 / math.sqrt(width)

    def kernel(half_ref, q_ref, k_ref, v_ref, o_ref):
        q = q_ref[:, 0].reshape(tile, width)
        scores = lax.dot_general(q, k_ref[...], (((1,), (1,)), ((), ())), preferred_element_type=F32)
        top = jnp.max(scores, axis=1, keepdims=True)
        probs = jnp.exp((scores - top) * scale)
        total = jnp.sum(probs, axis=1, keepdims=True)
        out = dot(probs.astype(BF16), v_ref[...]) / total
        level = top * scale + jnp.log(total)
        for b in range(tile_blocks):
            part = slice(b * pairs_block, (b + 1) * pairs_block)
            o_ref[b, 0:pairs_block, :] = out[part].astype(BF16)
            row = as_row(level[part], width)
            o_ref[b, pairs_block : pairs_block + STATS, :] = stacked(pieces(row), width).astype(BF16)

    return pl.pallas_call(
        kernel,
        grid_spec=pltpu.PrefetchScalarGridSpec(
            num_scalar_prefetch=1,
            grid=(steps,),
            in_specs=[
                pl.BlockSpec((tile_units, 1, unit, width), lambda i, half: (i, half[0], 0, 0)),
                pl.BlockSpec((length, width), lambda i, half: (0, 0)),
                pl.BlockSpec((length, width), lambda i, half: (0, 0)),
            ],
            out_specs=pl.BlockSpec((tile_blocks, pairs_block + STATS, width), lambda i, half: (i, 0, 0)),
        ),
        out_shape=jax.ShapeDtypeStruct((blocks, pairs_block + STATS, width), BF16),
        compiler_params=pltpu.CompilerParams(vmem_limit_bytes=48 << 20),
        name="attend",
    )(half, queries, keys, values)


def levels_of(ref, pairs_block):
    stats = ref[:, pairs_block : pairs_block + STATS, :].astype(F32)
    return stats[:, 0, :] + stats[:, 1, :] + stats[:, 2, :]


def merge_pair(mine, other, residual, names):
    blocks, height, width = mine.shape
    pairs_block = height - STATS

    def kernel(a_ref, b_ref, r_ref, n_ref, o_ref):
        level_a, level_b = levels_of(a_ref, pairs_block), levels_of(b_ref, pairs_block)
        top = jnp.maximum(level_a, level_b)
        share_a, share_b = jnp.exp(level_a - top), jnp.exp(level_b - top)
        total = share_a + share_b
        share_a, share_b = share_a / total, share_b / total
        level = top + jnp.log(total)
        first, second, third = pieces(level)
        residual_all = r_ref[...].astype(F32)
        listed = n_ref[...]
        for b in range(blocks):
            col_a, col_b = as_column(share_a[b : b + 1], pairs_block), as_column(share_b[b : b + 1], pairs_block)
            both = a_ref[b, 0:pairs_block, :].astype(F32) * col_a + b_ref[b, 0:pairs_block, :].astype(F32) * col_b
            o_ref[b, 0:pairs_block, :] = both.astype(BF16)
            own = residual_all[:, b * width : (b + 1) * width]
            rows = (first[b : b + 1], second[b : b + 1], third[b : b + 1], own[0:1], own[1:2], listed)
            o_ref[b, pairs_block:height, :] = stacked(rows, width).astype(BF16)

    return pl.pallas_call(
        kernel, out_shape=jax.ShapeDtypeStruct((blocks, height, width), BF16), name="merge_pair"
    )(mine, other, residual, names)


def combine_all(parts, rows_half, heads):
    sources, height, width = parts.shape
    pairs_block = height - STATS

    def kernel(x_ref, o_ref, acc_ref):
        level = levels_of(x_ref, pairs_block)
        share = jnp.exp(level - jnp.max(level, axis=0, keepdims=True))
        share = share / jnp.sum(share, axis=0, keepdims=True)
        acc = jnp.zeros((pairs_block, width), F32)
        for s in range(sources):
            acc = acc + x_ref[s, 0:pairs_block, :].astype(F32) * as_column(share[s : s + 1], pairs_block)
        acc_ref[...] = acc
        by_head = [acc_ref[pl.ds(h, rows_half, stride=heads), :] for h in range(heads)]
        attended = jnp.concatenate(by_head, axis=0).astype(BF16)
        for s in range(sources):
            o_ref[s] = attended

    return pl.pallas_call(
        kernel,
        out_shape=jax.ShapeDtypeStruct((sources, pairs_block, width), BF16),
        scratch_shapes=[pltpu.VMEM((pairs_block, width), F32)],
        name="combine_all",
    )(parts)


def project(attended, weight, parts, place, rows_half, heads, copies):
    blocks, pairs_block, width = attended.shape
    columns = weight.shape[1]
    rows = blocks * rows_half

    def kernel(place_ref, a_ref, w_ref, s_ref, o_ref):
        a = a_ref[...].astype(F32)
        by_head = [a[:, h * rows_half : (h + 1) * rows_half, :].reshape(rows, width) for h in range(heads)]
        out = dot(jnp.concatenate(by_head, axis=1).astype(BF16), w_ref[...])
        out = out.reshape(blocks, rows_half, columns)
        stats = s_ref[...].astype(F32)
        at = iota((blocks, rows_half, columns), 1)
        first = 2 * place_ref[0]
        out = out + jnp.where(at == first, stats[:, 3:4, :], 0.0) + jnp.where(at == first + 1, stats[:, 4:5, :], 0.0)
        out = out.reshape(rows, columns).astype(BF16)
        for i in range(copies):
            o_ref[i] = out

    height = parts.shape[1]
    return pl.pallas_call(
        kernel,
        grid_spec=pltpu.PrefetchScalarGridSpec(
            num_scalar_prefetch=1,
            grid=(1,),
            in_specs=[
                pl.BlockSpec(attended.shape, lambda i, place: (0, 0, 0)),
                pl.BlockSpec(weight.shape, lambda i, place: (0, 0)),
                pl.BlockSpec((blocks, STATS, width), lambda i, place: (0, (height - STATS) // STATS, 0)),
            ],
            out_specs=pl.BlockSpec((copies, rows, columns), lambda i, place: (0, 0, 0)),
        ),
        out_shape=jax.ShapeDtypeStruct((copies, rows, columns), BF16),
        name="project",
    )(place, attended, weight, parts)


def selection(parts, place, sizes):
    n_ctx, n_head, n_pair, rows_own, top, capacity = sizes
    block_rows = n_head * n_pair * rows_own
    rows_all = n_ctx * block_rows
    blocks, height, width = parts.shape
    per_peer = n_ctx * capacity
    owned = 8

    def natural(lane):
        pair = lane // (rows_all // n_pair)
        rest = lane % (rows_all // n_pair)
        block = rest // (n_head * rows_own)
        head = (rest // rows_own) % n_head
        return block, (head * n_pair + pair) * rows_own + rest % rows_own

    def kernel(place_ref, s_ref, d_ref, o_ref):
        listed = s_ref[...].astype(F32)[:, 5, :]
        count = n_ctx * n_ctx
        repeated = jnp.concatenate([listed] * n_ctx, axis=0)
        expert = (iota((count, width), 0) // n_ctx * n_head * n_pair + place_ref[0] * n_pair + place_ref[1]).astype(F32)
        equal = (repeated == expert).astype(F32).astype(BF16)
        fold = (iota((width, block_rows), 0) // top == iota((width, block_rows), 1)).astype(F32).astype(BF16)
        hits = dot(equal, fold)
        earlier = (iota((block_rows, block_rows), 0) < iota((block_rows, block_rows), 1)).astype(F32).astype(BF16)
        rank = dot(hits.astype(BF16), earlier)
        slot = jnp.where(hits > 0.5, rank + 1.0, 0.0).astype(BF16)
        expand = iota((count * capacity, count), 0) // capacity == iota((count * capacity, count), 1)
        slot = dot(expand.astype(F32).astype(BF16), slot).astype(BF16)
        block, row = natural(iota((block_rows, rows_all), 1))
        spread = (iota((block_rows, rows_all), 0) == row).astype(F32).astype(BF16)
        slot = dot(slot, spread)
        at = iota((count * capacity, rows_all), 0)
        block, row = natural(iota((count * capacity, rows_all), 1))
        mine = (block == (at // capacity) % n_ctx) & (slot == (at % capacity + 1).astype(F32))
        d_ref[...] = mine.astype(F32).astype(BF16)
        at = iota((n_ctx * owned, rows_all), 0)
        block, row = natural(iota((n_ctx * owned, rows_all), 1))
        first = (place_ref[0] * n_pair + place_ref[1]) * rows_own
        mine = (block == at // owned) & (row == first + at % owned) & (at % owned < rows_own)
        o_ref[...] = mine.astype(F32).astype(BF16)

    return pl.pallas_call(
        kernel,
        grid_spec=pltpu.PrefetchScalarGridSpec(
            num_scalar_prefetch=1,
            grid=(1,),
            in_specs=[pl.BlockSpec((blocks, STATS, width), lambda i, place: (0, (height - STATS) // STATS, 0))],
            out_specs=[
                pl.BlockSpec((n_ctx * per_peer, rows_all), lambda i, place: (0, 0)),
                pl.BlockSpec((n_ctx * owned, rows_all), lambda i, place: (0, 0)),
            ],
        ),
        out_shape=[
            jax.ShapeDtypeStruct((n_ctx * per_peer, rows_all), BF16),
            jax.ShapeDtypeStruct((n_ctx * owned, rows_all), BF16),
        ],
        name="selection",
    )(place, parts)


def dispatch(partials, picks, owns, n_ctx, n_head, n_pair):
    copies, rows, columns = partials.shape
    per_peer, owned = picks.shape[0] // n_ctx, owns.shape[0] // n_ctx

    def kernel(x_ref, d_ref, w_ref, o_ref):
        halves = []
        for p in range(n_pair):
            acc = x_ref[p].astype(F32)
            for h in range(1, n_head):
                acc = acc + x_ref[h * n_pair + p].astype(F32)
            halves.append(acc)
        hidden = jnp.concatenate(halves, axis=0).astype(BF16)
        sent = dot(d_ref[...], hidden).reshape(n_ctx, per_peer, columns)
        kept = dot(w_ref[...], hidden).reshape(n_ctx, owned, columns)
        o_ref[:, 0:per_peer, :] = sent.astype(BF16)
        o_ref[:, per_peer : per_peer + owned, :] = kept.astype(BF16)

    return pl.pallas_call(
        kernel, out_shape=jax.ShapeDtypeStruct((n_ctx, per_peer + owned, columns), BF16), name="dispatch"
    )(partials, picks, owns)


def norm_rows(parts, gain, per_peer):
    sources, height, columns = parts.shape
    owned = height - per_peer
    width = sources * columns

    def kernel(x_ref, g_ref, n_ref, o_ref):
        whole = jnp.concatenate([x_ref[s].astype(F32) for s in range(sources)], axis=1)
        o_ref[...] = whole[per_peer:height]
        rows = whole[0:per_peer]
        mean = jnp.sum(rows * rows, axis=1, keepdims=True) * (1.0 / width)
        n_ref[...] = (rows * lax.rsqrt(mean + 1e-06) * g_ref[...]).astype(BF16)

    return pl.pallas_call(
        kernel,
        out_shape=[jax.ShapeDtypeStruct((per_peer, width), BF16), jax.ShapeDtypeStruct((owned, width), F32)],
        name="norm_rows",
    )(parts, gain.reshape(1, width))


def weigh(returned, lists, weights, place, sizes):
    n_ctx, n_head, n_pair, rows_own, top, capacity = sizes
    slots, width = returned.shape
    rows = lists.shape[0]

    def kernel(place_ref, x_ref, l_ref, g_ref, o_ref):
        lane = iota((rows, slots), 1)
        expert = lane // capacity * n_head * n_pair + place_ref[0] * n_pair + place_ref[1]
        hits = jnp.zeros((rows, slots), F32)
        factor = jnp.zeros((rows, slots), F32)
        for k in range(top):
            same = l_ref[:, k : k + 1] == expert
            hits = jnp.where(same, 1.0, hits)
            factor = jnp.where(same, g_ref[:, k : k + 1], factor)
        earlier = (iota((rows, rows), 1) < iota((rows, rows), 0)).astype(F32).astype(BF16)
        rank = dot(earlier, hits.astype(BF16))
        factor = jnp.where(rank == (lane % capacity).astype(F32), factor, 0.0)
        first, second, third = pieces(factor)
        x = x_ref[...]
        o_ref[...] = dot(first.astype(BF16), x) + dot(second.astype(BF16), x) + dot(third.astype(BF16), x)

    return pl.pallas_call(
        kernel,
        grid_spec=pltpu.PrefetchScalarGridSpec(
            num_scalar_prefetch=1,
            grid=(1,),
            in_specs=[
                pl.BlockSpec((slots, width), lambda i, place: (0, 0)),
                pl.BlockSpec((rows, top), lambda i, place: (0, 0)),
                pl.BlockSpec((rows, top), lambda i, place: (0, 0)),
            ],
            out_specs=pl.BlockSpec((rows, width), lambda i, place: (0, 0)),
        ),
        out_shape=jax.ShapeDtypeStruct((rows, width), F32),
        name="weigh",
    )(place, returned, lists, weights)


def body(
    queries,
    prompt_keys,
    prompt_values,
    residual,
    out_weight,
    norm_gain,
    expert_lists,
    gate_weights,
    gate_up,
    down_proj,
):
    n_ctx = lax.axis_size("ctx")
    n_head = lax.axis_size("head")
    n_pair = lax.axis_size("pair")
    rows_own, width = residual.shape
    rows_all, heads, head_size = queries.shape
    block_rows, top = expert_lists.shape
    capacity = 2
    rows_half = n_head * rows_own
    pairs_block = rows_half * heads
    sizes = (n_ctx, n_head, n_pair, rows_own, top, capacity)
    head, pair = lax.axis_index("head"), lax.axis_index("pair")
    place = jnp.stack([head, pair]).astype(jnp.int32)

    units = queries.reshape(n_ctx * n_head, n_pair, rows_own * heads, head_size)
    keys = prompt_keys.reshape(-1, head_size)
    values = prompt_values.reshape(-1, head_size)
    theirs = attend_half((1 - pair).reshape(1), units, keys, values, n_ctx, pairs_block)
    swapped = lax.ppermute(theirs, "pair", [(0, 1), (1, 0)])
    ours = attend_half(pair.reshape(1), units, keys, values, n_ctx, pairs_block)
    names = expert_lists.astype(F32).reshape(1, block_rows * top)
    merged = merge_pair(ours, swapped, residual, names)
    parts = lax.all_to_all(merged, "ctx", 0, 0, tiled=True)
    copies = combine_all(parts, rows_half, heads)
    picks, owns = selection(parts, place, sizes)
    attended = lax.all_to_all(copies, "ctx", 0, 0, tiled=True)
    partial = project(attended, out_weight, parts, place, rows_half, heads, n_head * n_pair)
    partials = lax.all_to_all(partial, ("head", "pair"), 0, 0, tiled=True)
    sending = dispatch(partials, picks, owns, n_ctx, n_head, n_pair)
    arrived = lax.all_to_all(sending, "ctx", 0, 0, tiled=True)
    normed, own = norm_rows(arrived, norm_gain, n_ctx * capacity)
    hidden_units = down_proj.shape[1]
    both = jnp.dot(normed, gate_up[0], preferred_element_type=F32)
    inner = (jax.nn.silu(both[:, :hidden_units]) * both[:, hidden_units:]).astype(BF16)
    produced = jnp.dot(inner, down_proj[0], preferred_element_type=F32).astype(BF16)
    returned = lax.all_to_all(produced.reshape(n_ctx, capacity, width), "ctx", 0, 0, tiled=True)
    weighted = weigh(returned.reshape(n_ctx * capacity, width), expert_lists, gate_weights, place, sizes)
    shares = lax.all_to_all(weighted.reshape(n_head * n_pair, rows_own, width), ("head", "pair"), 0, 0, tiled=True)
    return (own[:rows_own] + jnp.sum(shares, axis=0)).astype(BF16)


def solution(mesh):
    in_specs = (
        P("groups", "head", None),
        P(("groups", "ctx", "pair"), "head", None),
        P(("groups", "ctx", "pair"), "head", None),
        P(("groups", "ctx", "head", "pair"), None),
        P("head", "ctx"),
        P(),
        P(("groups", "ctx"), None),
        P(("groups", "ctx"), None),
        P(("ctx", "head", "pair"), None, None),
        P(("ctx", "head", "pair"), None, None),
    )
    out_specs = P(("groups", "ctx", "head", "pair"), None)
    return jax.shard_map(body, mesh=mesh, in_specs=in_specs, out_specs=out_specs, check_vma=False)
```

time: 264 us -> 172 us (0.65)
  waiting for transfers between devices: 112 us -> 27.1 us
  matrix products: 32.4 us -> 4.62 us
  Pallas kernels: 0 us -> 25.2 us
  blocking collectives: 26.1 us -> 48.5 us
  between operations: 13.7 us -> 0.08 us
  other arithmetic: 11.4 us -> 2.79 us
  starting transfers between devices: 54.3 us -> 49.6 us
    all_to_all x6 -> x3, waiting for transfers between devices: 111 us -> 27.1 us  [the longest x1 13 us: body(): attended = lax.all_to_all(copies, 'ctx', 0, 0, tiled=True)]
    all_to_all x1 -> x3, blocking collectives: 11.5 us -> 48.5 us  [the longest x1 19.1 us: body(): parts = lax.all_to_all(merged, 'ctx', 0, 0, tiled=True)]
    dot_general x8 -> x2, matrix products: 32.4 us -> 4.62 us  [the longest x1 4 us: body(): both = jnp.dot(normed, gate_up[0], preferred_element_type=F32)]
    pallas_call x0 -> x9, Pallas kernels: none -> 25.2 us  [the longest x2 9.43 us: attend_half(): pl.pallas_call(kernel, grid_spec=pltpu.PrefetchScalarGridSpec(num_scalar_...]
    all_to_all x6 -> x3, starting transfers between devices: 54.3 us -> 29.1 us  [the longest x1 11.5 us: body(): attended = lax.all_to_all(copies, 'ctx', 0, 0, tiled=True)]
    ppermute x0 -> x1, starting transfers between devices: none -> 20.5 us  [body(): swapped = lax.ppermute(theirs, 'pair', [(0, 1), (1, 0)])]
    all_gather x1 -> x0, blocking collectives: 14.6 us -> none  [body(): block_rows = lax.all_gather(normed, ('head', 'pair'), axis=0, tiled=True)]
    reduce_sum x9 -> x1, other arithmetic: 8.02 us -> 0.05 us  [body(): return (own[:rows_own] + jnp.sum(shares, axis=0)).astype(BF16)]
  transfers between devices with their start and end apart: 7 -> 4, of which waited for: 6 -> 3; matrix products, arithmetic and copies ran while one was open for 15% -> 2% of each run, Pallas kernels for 0% -> 4%
where the time goes in v1:
time: 172 us; the launch traced here: 171 us
  starting transfers between devices  49.6 us (29%)
  blocking collectives  48.5 us (28%)
  waiting for transfers between devices  27.1 us (16%)
  Pallas kernels  25.2 us (15%)
  local copies, waits for them, and re-layouts  13 us (8%)
  matrix products  4.62 us (3%)
  other arithmetic  2.79 us (2%)
    ppermute x1, starting transfers between devices, body(): swapped = lax.ppermute(theirs, 'pair', [(0, 1), (1, 0)])  20.5 us
    all_to_all x1, blocking collectives, body(): parts = lax.all_to_all(merged, 'ctx', 0, 0, tiled=True)  19.1 us
    all_to_all x1, blocking collectives, body(): arrived = lax.all_to_all(sending, 'ctx', 0, 0, tiled=True)  17.9 us
    all_to_all x1, waiting for transfers between devices, body(): attended = lax.all_to_all(copies, 'ctx', 0, 0, tiled=True)  13 us
    all_to_all x1, blocking collectives, body(): lax.all_to_all(weighted.reshape(n_head * n_pair, rows_own, width), ('head...  11.5 us
    all_to_all x1, starting transfers between devices, body(): attended = lax.all_to_all(copies, 'ctx', 0, 0, tiled=True)  11.5 us
    all_to_all x1, waiting for transfers between devices, body(): lax.all_to_all(produced.reshape(n_ctx, capacity, width), 'ctx', 0, 0, til...  10.4 us
    all_to_all x1, starting transfers between devices, body(): partials = lax.all_to_all(partial, ('head', 'pair'), 0, 0, tiled=True)  10.1 us
  transfers between devices with their start and end apart: 4, of which 3 were waited for; matrix products, arithmetic and copies ran while one was open for 2% of the time, Pallas kernels for 4%

profile of v1, /device:TPU:33, one launch (start us, length us, event | category | flops | bytes accessed | tf_op | source)
XLA Modules:
  0.0 170.9 jit_solution(9142171876020631229)
XLA Ops:
  0.0 0.0 copy-start
  0.0 0.0 copy-start.1
  0.0 1.2 copy-done.1
  1.2 0.0 copy-start.3
  1.2 1.0 copy-done.3
  2.2 0.0 copy-start.5
  2.2 1.0 copy-done.5
  3.3 4.7 %attend.3 = bf16[16,72,128]{2,1,0:T(8,128)(2,1)S(1)} custom-call(s32[1]{0:T(128)} %bitcast.5.half_ref, bf16[64,2,16,128]{3,2,1,0:T(8,128)(2,1)S(1)} %bitcast.16, bf16[2048,128]{1,0:T(8,128)(2,1)S(1)} %bitcast.18, bf16[2048,128]{1,0:T(8,128)(2,1)S(1)} %bitcast.20), custom_call_target="tpu_custom_call" | custom-call | tf_op jit(solution)/shard_map/attend/pallas_call | solution.py:73
  8.0 20.5 %collective-permute-start = (bf16[16,72,128]{2,1,0:T(8,128)(2,1)S(1)}, bf16[16,72,128]{2,1,0:T(8,128)(2,1)}, u32[]{:S(2)}, u32[]{:S(2)}) collective-permute-start(bf16[16,72,128]{2,1,0:T(8,128)(2,1)S(1)} %attend.3), channel_id=1, source_target_pairs={{0,1},{1,0},{2,3},{3,2},{4,5},{5,4},{6,7},{7,6},{8,9},{9,8},{10,11... | collective-permute-start | bytes 884744 | tf_op jit(solution)/shard_map/ppermute | solution.py:352
  28.5 0.0 copy-start.2
  28.5 1.0 copy-done.2
  29.5 0.0 copy-start.4
  29.5 1.0 copy-done.4
  30.6 0.0 copy-start.6
  30.6 1.0 copy-done.6
  31.6 4.7 %attend.2.a_ref = bf16[16,72,128]{2,1,0:T(8,128)(2,1)S(1)} custom-call(s32[1]{0:T(128)} %bitcast.1.half_ref, bf16[64,2,16,128]{3,2,1,0:T(8,128)(2,1)S(1)} %bitcast.17, bf16[2048,128]{1,0:T(8,128)(2,1)S(1)} %bitcast.19, bf16[2048,128]{1,0:T(8,128)(2,1)S(1)} %bitcast.21), custom_call_target="tpu_custom_call" | custom-call | tf_op jit(solution)/shard_map/attend/pallas_call | solution.py:73
  36.3 0.0 copy-start.7
  36.3 0.7 copy-done.7
  37.0 0.7 convert_element_type.12
  37.7 0.1 copy.14
  37.8 0.6 reshape.32.n_ref
  38.4 0.0 collective-permute-done.b_ref
  38.4 2.2 %merge_pair.1 = bf16[16,72,128]{2,1,0:T(8,128)(2,1)} custom-call(bf16[16,72,128]{2,1,0:T(8,128)(2,1)} %copy-done.7, bf16[16,72,128]{2,1,0:T(8,128)(2,1)} %collective-permute-done.b_ref, bf16[2,2048]{1,0:T(2,128)(2,1)} %r_ref.1, f32[1,128]{1,0:T(1,128)} %reshape.32.n_ref), custom_call_target="tpu_custom_call" | custom-call | tf_op jit(solution)/shard_map/merge_pair/pallas_call | solution.py:118
  40.6 19.1 %all_to_all.30.x_ref.s_ref = bf16[16,72,128]{2,1,0:T(8,128)(2,1)} all-to-all(bf16[16,72,128]{2,1,0:T(8,128)(2,1)} %merge_pair.1), channel_id=1, replica_groups=mesh['groups'=2,'ctx'=16,'head'=4,'pair'=2] {'ctx'}, dimensions={0} | all-to-all | bytes 589824 | tf_op jit(solution)/shard_map/all_to_all | solution.py:356
  59.7 1.9 %combine_all.1 = bf16[16,64,128]{2,1,0:T(8,128)(2,1)} custom-call(bf16[16,72,128]{2,1,0:T(8,128)(2,1)} %all_to_all.30.x_ref.s_ref), custom_call_target="tpu_custom_call" | custom-call | tf_op jit(solution)/shard_map/combine_all/pallas_call | solution.py:140
  61.6 11.5 %all-to-all-start.1 = ((bf16[16,64,128]{2,1,0:T(8,128)(2,1)}), bf16[16,64,128]{2,1,0:T(8,128)(2,1)S(1)}, u32[]{:S(2)}, u32[]{:S(2)}) async-start(bf16[16,64,128]{2,1,0:T(8,128)(2,1)} %combine_all.1), calls=%async_computation.1 | async-start | bytes 524288 | tf_op jit(solution)/shard_map/all_to_all | solution.py:359
  73.1 0.6 pad_add_fusion.place_ref
  73.7 13.0 %all-to-all-done.1.a_ref = bf16[16,64,128]{2,1,0:T(8,128)(2,1)S(1)} async-done(((bf16[16,64,128]{2,1,0:T(8,128)(2,1)}), bf16[16,64,128]{2,1,0:T(8,128)(2,1)S(1)}, u32[]{:S(2)}, u32[]{:S(2)}) %all-to-all-start.1) | async-done | bytes 262176 | tf_op jit(solution)/shard_map/all_to_all | solution.py:359
  86.7 0.0 copy-start.9
  86.7 0.7 copy-done.9
  87.4 2.6 %project.1 = bf16[8,128,128]{2,1,0:T(8,128)(2,1)} custom-call(s32[2]{0:T(128)} %pad_add_fusion.place_ref, bf16[16,64,128]{2,1,0:T(8,128)(2,1)} %copy-done.9, bf16[1024,128]{1,0:T(8,128)(2,1)} %w_ref.1, bf16[16,72,128]{2,1,0:T(8,128)(2,1)} %all_to_all.30.x_ref.s_ref), custom_call_target="tpu_custom_call" | custom-call | tf_op jit(solution)/shard_map/project/pallas_call | solution.py:167
  90.0 0.0 copy-start.10
  90.0 0.0 copy-start.11
  90.0 10.1 %all-to-all-start.2 = ((bf16[8,128,128]{2,1,0:T(8,128)(2,1)}), bf16[8,128,128]{2,1,0:T(8,128)(2,1)S(1)}, u32[]{:S(2)}, u32[]{:S(2)}) async-start(bf16[8,128,128]{2,1,0:T(8,128)(2,1)} %project.1), calls=%async_computation.2 | async-start | bytes 524288 | tf_op jit(solution)/shard_map/all_to_all | solution.py:361
  100.1 2.8 %selection.1 = (bf16[512,256]{1,0:T(8,128)(2,1)}, bf16[128,256]{1,0:T(8,128)(2,1)}) custom-call(s32[2]{0:T(128)} %pad_add_fusion.place_ref, bf16[16,72,128]{2,1,0:T(8,128)(2,1)} %all_to_all.30.x_ref.s_ref), custom_call_target="tpu_custom_call" | custom-call | tf_op jit(solution)/shard_map/selection/pallas_call | solution.py:225
  102.9 3.7 %all-to-all-done.2.x_ref = bf16[8,128,128]{2,1,0:T(8,128)(2,1)S(1)} async-done(((bf16[8,128,128]{2,1,0:T(8,128)(2,1)}), bf16[8,128,128]{2,1,0:T(8,128)(2,1)S(1)}, u32[]{:S(2)}, u32[]{:S(2)}) %all-to-all-start.2) | async-done | bytes 262176 | tf_op jit(solution)/shard_map/all_to_all | solution.py:361
  106.5 0.0 copy-start.8
  106.5 0.7 copy-done.8
  107.3 2.0 %dispatch.1 = bf16[16,40,128]{2,1,0:T(8,128)(2,1)} custom-call(bf16[8,128,128]{2,1,0:T(8,128)(2,1)} %copy-done.8, bf16[512,256]{1,0:T(8,128)(2,1)} %get-tuple-element.9.d_ref, bf16[128,256]{1,0:T(8,128)(2,1)} %get-tuple-element.10.w_ref), custom_call_target="tpu_custom_call" | custom-call | tf_op jit(solution)/shard_map/dispatch/pallas_call | solution.py:261
  109.2 17.9 %all_to_all.31.x_ref = bf16[16,40,128]{2,1,0:T(8,128)(2,1)} all-to-all(bf16[16,40,128]{2,1,0:T(8,128)(2,1)} %dispatch.1), channel_id=1, replica_groups=mesh['groups'=2,'ctx'=16,'head'=4,'pair'=2] {'ctx'}, dimensions={0} | all-to-all | bytes 327680 | tf_op jit(solution)/shard_map/all_to_all | solution.py:363
  127.1 1.7 %norm_rows.1 = (bf16[32,2048]{1,0:T(8,128)(2,1)}, f32[8,2048]{1,0:T(8,128)}) custom-call(bf16[16,40,128]{2,1,0:T(8,128)(2,1)} %all_to_all.31.x_ref, f32[1,2048]{1,0:T(1,128)} %bitcast.22), custom_call_target="tpu_custom_call" | custom-call | tf_op jit(solution)/shard_map/norm_rows/pallas_call | solution.py:278
  128.8 4.0 %fusion = f32[32,1536]{1,0:T(8,128)S(1)} fusion(bf16[32,2048]{1,0:T(8,128)(2,1)} %get-tuple-element.12, bf16[1,2048,1536]{2,1,0:T(8,128)(2,1)} %param.18), kind=kOutput, calls=%fused_computation | convolution fusion | flops 201326592 | bytes 6619136 | tf_op jit(solution)/shard_map/dot_general | solution.py:366
  132.8 0.0 copy-done
  132.8 0.6 fusion.4
  133.4 0.8 reshape.34
  134.2 7.6 %all-to-all-start.4 = ((bf16[16,2,2048]{2,1,0:T(2,128)(2,1)}), bf16[16,2,2048]{2,1,0:T(2,128)(2,1)S(1)}, u32[]{:S(2)}, u32[]{:S(2)}) async-start(bf16[16,2,2048]{2,1,0:T(2,128)(2,1)} %reshape.34), calls=%async_computation.4 | async-start | bytes 262144 | tf_op jit(solution)/shard_map/all_to_all | solution.py:369
  141.8 0.0 copy-done.10
  141.8 0.7 copy.15.l_ref
  142.5 0.0 copy-done.11
  142.5 0.7 copy.16.g_ref
  143.2 10.4 %all-to-all-done.4 = bf16[16,2,2048]{2,1,0:T(2,128)(2,1)S(1)} async-done(((bf16[16,2,2048]{2,1,0:T(2,128)(2,1)}), bf16[16,2,2048]{2,1,0:T(2,128)(2,1)S(1)}, u32[]{:S(2)}, u32[]{:S(2)}) %all-to-all-start.4) | async-done | bytes 131104 | tf_op jit(solution)/shard_map/all_to_all | solution.py:369
  153.6 0.7 reshape.35.x_ref
  154.3 2.6 %weigh.1 = f32[16,2048]{1,0:T(8,128)} custom-call(s32[2]{0:T(128)} %pad_add_fusion.place_ref, bf16[32,2048]{1,0:T(8,128)(2,1)} %reshape.35.x_ref, s32[16,8]{1,0:T(8,128)} %copy.15.l_ref, f32[16,8]{1,0:T(8,128)} %copy.16.g_ref), custom_call_target="tpu_custom_call" | custom-call | tf_op jit(solution)/shard_map/weigh/pallas_call | solution.py:306
  156.9 1.0 reshape.36
  157.9 11.5 %all_to_all.32 = f32[8,2,2048]{2,1,0:T(2,128)S(1)} all-to-all(f32[8,2,2048]{2,1,0:T(2,128)S(1)} %reshape.36), channel_id=1, replica_groups=mesh['groups'=2,'ctx'=16,'head'=4,'pair'=2] {'head','pair'}, dimensions={0} | all-to-all | bytes 262144 | tf_op jit(solution)/shard_map/all_to_all | solution.py:371
  169.5 1.4 add_convert_fusion
  (1 shorter events, 0.0 us)
Async XLA Ops:
  0.0 132.8 %copy-start = (bf16[1,768,2048]{2,1,0:T(8,128)(2,1)S(1)}, bf16[1,768,2048]{2,1,0:T(8,128)(2,1)}, u32[]{:S(2)}) copy-start(bf16[1,768,2048]{2,1,0:T(8,128)(2,1)} %param.19) | copy-start | bytes 9437188
  0.0 1.2 copy-start.1
  1.2 1.0 copy-start.3
  2.2 1.0 copy-start.5
  8.0 30.4 %collective-permute-start = (bf16[16,72,128]{2,1,0:T(8,128)(2,1)S(1)}, bf16[16,72,128]{2,1,0:T(8,128)(2,1)}, u32[]{:S(2)}, u32[]{:S(2)}) collective-permute-start(bf16[16,72,128]{2,1,0:T(8,128)(2,1)S(1)} %attend.3), channel_id=1, source_target_pairs={{0,1},{1,0},{2,3},{3,2},{4,5},{5,4},{6,7},{7,6},{8,9},{9,8},{10,11... | collective-permute-start | bytes 884744 | tf_op jit(solution)/shard_map/ppermute | solution.py:352
  28.5 1.0 copy-start.2
  29.5 1.0 copy-start.4
  30.6 1.0 copy-start.6
  36.3 0.7 copy-start.7
  61.6 25.1 %all-to-all-start.1 = ((bf16[16,64,128]{2,1,0:T(8,128)(2,1)}), bf16[16,64,128]{2,1,0:T(8,128)(2,1)S(1)}, u32[]{:S(2)}, u32[]{:S(2)}) async-start(bf16[16,64,128]{2,1,0:T(8,128)(2,1)} %combine_all.1), calls=%async_computation.1 | async-start | bytes 524288 | tf_op jit(solution)/shard_map/all_to_all | solution.py:359
  86.7 0.7 copy-start.9
  90.0 51.8 %copy-start.10 = (s32[16,8]{0,1:T(8,128)S(1)}, s32[16,8]{0,1:T(8,128)}, u32[]{:S(2)}) copy-start(s32[16,8]{0,1:T(8,128)} %param.16) | copy-start | bytes 1540
  90.0 52.5 %copy-start.11 = (f32[16,8]{0,1:T(8,128)S(1)}, f32[16,8]{0,1:T(8,128)}, u32[]{:S(2)}) copy-start(f32[16,8]{0,1:T(8,128)} %param.17) | copy-start | bytes 1540
  90.0 16.5 %all-to-all-start.2 = ((bf16[8,128,128]{2,1,0:T(8,128)(2,1)}), bf16[8,128,128]{2,1,0:T(8,128)(2,1)S(1)}, u32[]{:S(2)}, u32[]{:S(2)}) async-start(bf16[8,128,128]{2,1,0:T(8,128)(2,1)} %project.1), calls=%async_computation.2 | async-start | bytes 524288 | tf_op jit(solution)/shard_map/all_to_all | solution.py:361
  106.5 0.7 copy-start.8
  134.2 19.3 %all-to-all-start.4 = ((bf16[16,2,2048]{2,1,0:T(2,128)(2,1)}), bf16[16,2,2048]{2,1,0:T(2,128)(2,1)S(1)}, u32[]{:S(2)}, u32[]{:S(2)}) async-start(bf16[16,2,2048]{2,1,0:T(2,128)(2,1)} %reshape.34), calls=%async_computation.4 | async-start | bytes 262144 | tf_op jit(solution)/shard_map/all_to_all | solution.py:369

commit v2 on v1

v2 whole, which is shorter than its diff:
```python
import math

import jax
import jax.numpy as jnp
from jax import lax
from jax.experimental import pallas as pl
from jax.experimental.pallas import tpu as pltpu
from jax.sharding import PartitionSpec as P

F32 = jnp.float32
BF16 = jnp.bfloat16
LIMIT = 16 << 20
STATS = 8


SMEM = pl.BlockSpec(memory_space=pltpu.SMEM)
VMEM = pl.BlockSpec(memory_space=pltpu.VMEM)
HBM = pl.BlockSpec(memory_space=pltpu.HBM)


def in_hbm(x):
    return pltpu.with_memory_space_constraint(x, pltpu.HBM)


def iota(shape, dim):
    return lax.broadcasted_iota(jnp.int32, shape, dim)


def dot(a, b):
    return lax.dot_general(a, b, (((1,), (0,)), ((), ())), preferred_element_type=F32)


def as_row(column, lanes):
    n = column.shape[0]
    here = iota((n, lanes), 0) == iota((n, lanes), 1)
    return jnp.sum(jnp.where(here, jnp.broadcast_to(column, (n, lanes)), 0.0), axis=0, keepdims=True)


def as_column(row, n):
    lanes = row.shape[1]
    here = iota((n, lanes), 0) == iota((n, lanes), 1)
    return jnp.sum(jnp.where(here, jnp.broadcast_to(row, (n, lanes)), 0.0), axis=1, keepdims=True)


def pieces(row):
    first = row.astype(BF16).astype(F32)
    second = (row - first).astype(BF16).astype(F32)
    third = row - first - second
    return first, second, third


def stacked(rows, lanes):
    at = iota((STATS, lanes), 0)
    out = jnp.zeros((STATS, lanes), F32)
    for i, row in enumerate(rows):
        out = jnp.where(at == i, jnp.broadcast_to(row, (STATS, lanes)), out)
    return out


def attend_half(half, queries, keys, values, blocks, pairs_block):
    units, _, unit, width = queries.shape
    length = keys.shape[0]
    tile_blocks = max(1, 256 // pairs_block)
    steps = blocks // tile_blocks
    tile_units = units // steps
    tile = tile_units * unit
    scale = 1.0 / math.sqrt(width)

    def kernel(half_ref, q_hbm, k_hbm, v_hbm, o_ref, q_ref, k_ref, v_ref, sems):
        copy_k = pltpu.make_async_copy(k_hbm, k_ref, sems.at[0])
        copy_q = pltpu.make_async_copy(q_hbm.at[:, half_ref[0]], q_ref, sems.at[1])
        copy_v = pltpu.make_async_copy(v_hbm, v_ref, sems.at[2])
        copy_q.start()
        copy_k.start()
        copy_v.start()
        copy_q.wait()
        copy_k.wait()
        copy_v.wait()

        def step(i, carry):
            q = q_ref[pl.ds(i * tile_units, tile_units)].reshape(tile, width)
            scores = lax.dot_general(q, k_ref[...], (((1,), (1,)), ((), ())), preferred_element_type=F32)
            top = jnp.max(scores, axis=1, keepdims=True)
            probs = jnp.exp((scores - top) * scale)
            total = jnp.sum(probs, axis=1, keepdims=True)
            out = dot(probs.astype(BF16), v_ref[...]) / total
            level = top * scale + jnp.log(total)
            for b in range(tile_blocks):
                part = slice(b * pairs_block, (b + 1) * pairs_block)
                at = i * tile_blocks + b
                o_ref[at, 0:pairs_block, :] = out[part].astype(BF16)
                row = as_row(level[part], width)
                o_ref[at, pairs_block : pairs_block + STATS, :] = stacked(pieces(row), width).astype(BF16)
            return carry

        lax.fori_loop(0, steps, step, 0)

    return pl.pallas_call(
        kernel,
        in_specs=[SMEM, HBM, HBM, HBM],
        out_specs=VMEM,
        out_shape=jax.ShapeDtypeStruct((blocks, pairs_block + STATS, width), BF16),
        scratch_shapes=[
            pltpu.VMEM((units, unit, width), BF16),
            pltpu.VMEM((length, width), BF16),
            pltpu.VMEM((length, width), BF16),
            pltpu.SemaphoreType.DMA((3,)),
        ],
        compiler_params=pltpu.CompilerParams(vmem_limit_bytes=24 << 20),
        name="attend",
    )(half, in_hbm(queries), in_hbm(keys), in_hbm(values))


def levels_of(ref, pairs_block):
    stats = ref[:, pairs_block : pairs_block + STATS, :].astype(F32)
    return stats[:, 0, :] + stats[:, 1, :] + stats[:, 2, :]


def merge_pair(mine, other, residual, names):
    blocks, height, width = mine.shape
    pairs_block = height - STATS

    def kernel(a_ref, b_ref, r_hbm, n_hbm, o_ref, r_ref, n_ref, sems):
        copy_r = pltpu.make_async_copy(r_hbm, r_ref, sems.at[0])
        copy_n = pltpu.make_async_copy(n_hbm, n_ref, sems.at[1])
        copy_r.start()
        copy_n.start()
        level_a, level_b = levels_of(a_ref, pairs_block), levels_of(b_ref, pairs_block)
        highest = jnp.maximum(level_a, level_b)
        share_a, share_b = jnp.exp(level_a - highest), jnp.exp(level_b - highest)
        total = share_a + share_b
        share_a, share_b = share_a / total, share_b / total
        level = highest + jnp.log(total)
        first, second, third = pieces(level)
        for b in range(blocks):
            col_a, col_b = as_column(share_a[b : b + 1], pairs_block), as_column(share_b[b : b + 1], pairs_block)
            both = a_ref[b, 0:pairs_block, :].astype(F32) * col_a + b_ref[b, 0:pairs_block, :].astype(F32) * col_b
            o_ref[b, 0:pairs_block, :] = both.astype(BF16)
        copy_r.wait()
        copy_n.wait()
        residual_all = r_ref[...].astype(F32)
        top, rows = n_ref.shape
        spread = (iota((rows, width), 1) % rows == iota((rows, width), 0)).astype(F32).astype(BF16)
        listed = dot(n_ref[...].astype(F32).astype(BF16), spread)
        listed = jnp.where(iota((top, width), 1) // rows == iota((top, width), 0), listed, 0.0)
        listed = jnp.sum(listed, axis=0, keepdims=True)
        for b in range(blocks):
            own = residual_all[:, b * width : (b + 1) * width]
            rows_b = (first[b : b + 1], second[b : b + 1], third[b : b + 1], own[0:1], own[1:2], listed)
            o_ref[b, pairs_block:height, :] = stacked(rows_b, width).astype(BF16)

    return pl.pallas_call(
        kernel,
        in_specs=[VMEM, VMEM, HBM, HBM],
        out_shape=jax.ShapeDtypeStruct((blocks, height, width), BF16),
        scratch_shapes=[
            pltpu.VMEM(residual.shape, residual.dtype),
            pltpu.VMEM(names.shape, names.dtype),
            pltpu.SemaphoreType.DMA((2,)),
        ],
        compiler_params=pltpu.CompilerParams(vmem_limit_bytes=LIMIT),
        name="merge_pair",
    )(mine, other, in_hbm(residual), in_hbm(names))


def combine_all(parts, rows_half, heads):
    sources, height, width = parts.shape
    pairs_block = height - STATS

    def kernel(x_ref, o_hbm, acc_ref, att_ref, sem):
        level = levels_of(x_ref, pairs_block)
        share = jnp.exp(level - jnp.max(level, axis=0, keepdims=True))
        share = share / jnp.sum(share, axis=0, keepdims=True)
        acc = jnp.zeros((pairs_block, width), F32)
        for s in range(sources):
            acc = acc + x_ref[s, 0:pairs_block, :].astype(F32) * as_column(share[s : s + 1], pairs_block)
        acc_ref[...] = acc
        by_head = [acc_ref[pl.ds(h, rows_half, stride=heads), :] for h in range(heads)]
        att_ref[...] = jnp.concatenate(by_head, axis=0).astype(BF16)
        copies = [pltpu.make_async_copy(att_ref, o_hbm.at[s], sem.at[s]) for s in range(sources)]
        for copy in copies:
            copy.start()
        for copy in copies:
            copy.wait()

    return pl.pallas_call(
        kernel,
        in_specs=[VMEM],
        out_specs=HBM,
        out_shape=pltpu.HBM((sources, pairs_block, width), BF16),
        scratch_shapes=[
            pltpu.VMEM((pairs_block, width), F32),
            pltpu.VMEM((pairs_block, width), BF16),
            pltpu.SemaphoreType.DMA((sources,)),
        ],
        compiler_params=pltpu.CompilerParams(vmem_limit_bytes=LIMIT),
        name="combine_all",
    )(parts)


def project(attended, weight, parts, place, rows_half, heads, copies):
    blocks, pairs_block, width = attended.shape
    columns = weight.shape[1]
    rows = blocks * rows_half

    def kernel(place_ref, a_ref, w_ref, s_ref, o_ref):
        a = a_ref[...].astype(F32)
        by_head = [a[:, h * rows_half : (h + 1) * rows_half, :].reshape(rows, width) for h in range(heads)]
        out = dot(jnp.concatenate(by_head, axis=1).astype(BF16), w_ref[...])
        out = out.reshape(blocks, rows_half, columns)
        stats = s_ref[:, pairs_block : pairs_block + STATS, :].astype(F32)
        at = iota((blocks, rows_half, columns), 1)
        first = 2 * place_ref[0]
        out = out + jnp.where(at == first, stats[:, 3:4, :], 0.0) + jnp.where(at == first + 1, stats[:, 4:5, :], 0.0)
        out = out.reshape(rows, columns).astype(BF16)
        for i in range(copies):
            o_ref[i] = out

    return pl.pallas_call(
        kernel,
        in_specs=[SMEM, VMEM, VMEM, VMEM],
        out_shape=jax.ShapeDtypeStruct((copies, rows, columns), BF16),
        compiler_params=pltpu.CompilerParams(vmem_limit_bytes=LIMIT),
        name="project",
    )(place, attended, weight, parts)


def selection(parts, place, sizes, fetched):
    n_ctx, n_head, n_pair, rows_own, top, capacity = sizes
    block_rows = n_head * n_pair * rows_own
    rows_all = n_ctx * block_rows
    blocks, height, width = parts.shape
    per_peer = n_ctx * capacity
    owned = 8

    def natural(lane):
        pair = lane // (rows_all // n_pair)
        rest = lane % (rows_all // n_pair)
        block = rest // (n_head * rows_own)
        head = (rest // rows_own) % n_head
        return block, (head * n_pair + pair) * rows_own + rest % rows_own

    count_fetched = len(fetched)

    def kernel(place_ref, s_ref, *refs):
        sources, d_ref, o_ref = refs[:count_fetched], refs[count_fetched], refs[count_fetched + 1]
        targets, sems = refs[count_fetched + 2 : -1], refs[-1]
        fetches = [pltpu.make_async_copy(a, b, sems.at[i]) for i, (a, b) in enumerate(zip(sources, targets))]
        for fetch in fetches:
            fetch.start()
        listed = s_ref[:, height - STATS : height, :].astype(F32)[:, 5, :]
        count = n_ctx * n_ctx
        repeated = jnp.concatenate([listed] * n_ctx, axis=0)
        expert = (iota((count, width), 0) // n_ctx * n_head * n_pair + place_ref[0] * n_pair + place_ref[1]).astype(F32)
        equal = (repeated == expert).astype(F32).astype(BF16)
        fold = (iota((width, block_rows), 0) % block_rows == iota((width, block_rows), 1)).astype(F32).astype(BF16)
        hits = dot(equal, fold)
        earlier = (iota((block_rows, block_rows), 0) < iota((block_rows, block_rows), 1)).astype(F32).astype(BF16)
        rank = dot(hits.astype(BF16), earlier)
        slot = jnp.where(hits > 0.5, rank + 1.0, 0.0).astype(BF16)
        expand = iota((count * capacity, count), 0) // capacity == iota((count * capacity, count), 1)
        slot = dot(expand.astype(F32).astype(BF16), slot).astype(BF16)
        block, row = natural(iota((block_rows, rows_all), 1))
        spread = (iota((block_rows, rows_all), 0) == row).astype(F32).astype(BF16)
        slot = dot(slot, spread)
        at = iota((count * capacity, rows_all), 0)
        block, row = natural(iota((count * capacity, rows_all), 1))
        mine = (block == (at // capacity) % n_ctx) & (slot == (at % capacity + 1).astype(F32))
        d_ref[...] = mine.astype(F32).astype(BF16)
        at = iota((n_ctx * owned, rows_all), 0)
        block, row = natural(iota((n_ctx * owned, rows_all), 1))
        first = (place_ref[0] * n_pair + place_ref[1]) * rows_own
        mine = (block == at // owned) & (row == first + at % owned) & (at % owned < rows_own)
        o_ref[...] = mine.astype(F32).astype(BF16)
        for fetch in fetches:
            fetch.wait()

    return pl.pallas_call(
        kernel,
        in_specs=[SMEM, VMEM] + [HBM] * count_fetched,
        out_specs=[VMEM] * (2 + count_fetched),
        out_shape=[
            jax.ShapeDtypeStruct((n_ctx * per_peer, rows_all), BF16),
            jax.ShapeDtypeStruct((n_ctx * owned, rows_all), BF16),
        ]
        + [jax.ShapeDtypeStruct(x.shape, x.dtype) for x in fetched],
        scratch_shapes=[pltpu.SemaphoreType.DMA((count_fetched,))],
        compiler_params=pltpu.CompilerParams(vmem_limit_bytes=LIMIT),
        name="selection",
    )(place, parts, *[in_hbm(x) for x in fetched])


def dispatch(partials, picks, owns, n_ctx, n_head, n_pair):
    copies, rows, columns = partials.shape
    per_peer, owned = picks.shape[0] // n_ctx, owns.shape[0] // n_ctx

    def kernel(x_ref, d_ref, w_ref, o_ref):
        halves = []
        for p in range(n_pair):
            acc = x_ref[p].astype(F32)
            for h in range(1, n_head):
                acc = acc + x_ref[h * n_pair + p].astype(F32)
            halves.append(acc)
        hidden = jnp.concatenate(halves, axis=0).astype(BF16)
        sent = dot(d_ref[...], hidden).reshape(n_ctx, per_peer, columns)
        kept = dot(w_ref[...], hidden).reshape(n_ctx, owned, columns)
        o_ref[:, 0:per_peer, :] = sent.astype(BF16)
        o_ref[:, per_peer : per_peer + owned, :] = kept.astype(BF16)

    return pl.pallas_call(
        kernel, out_shape=jax.ShapeDtypeStruct((n_ctx, per_peer + owned, columns), BF16), compiler_params=pltpu.CompilerParams(vmem_limit_bytes=LIMIT), name="dispatch"
    )(partials, picks, owns)


def run_expert(parts, gain, gate_up, down, capacity):
    sources, height, columns = parts.shape
    slots = sources * capacity
    owned = height - slots
    width = sources * columns
    units = down.shape[0]
    chunks = 8
    chunk = width // chunks

    def kernel(x_ref, g_ref, up_hbm, down_hbm, y_ref, o_ref, up_ref, down_ref, sems):
        ups = [
            pltpu.make_async_copy(
                up_hbm.at[pl.ds(i * chunk, chunk)], up_ref.at[pl.ds(i * chunk, chunk)], sems.at[i]
            )
            for i in range(chunks)
        ]
        last = pltpu.make_async_copy(down_hbm, down_ref, sems.at[chunks])
        for copy in ups:
            copy.start()
        last.start()
        whole = jnp.concatenate([x_ref[s].astype(F32) for s in range(sources)], axis=1)
        o_ref[...] = whole[slots:height]
        rows = whole[0:slots]
        mean = jnp.sum(rows * rows, axis=1, keepdims=True) * (1.0 / width)
        normed = (rows * lax.rsqrt(mean + 1e-06) * g_ref[...]).astype(BF16)
        both = jnp.zeros((slots, 2 * units), F32)
        for i in range(chunks):
            ups[i].wait()
            both = both + dot(normed[:, i * chunk : (i + 1) * chunk], up_ref[i * chunk : (i + 1) * chunk, :])
        gate = both[:, :units]
        inner = (gate / (1.0 + jnp.exp(-gate)) * both[:, units:]).astype(BF16)
        last.wait()
        y_ref[...] = dot(inner, down_ref[...]).astype(BF16).reshape(sources, capacity, width)

    return pl.pallas_call(
        kernel,
        in_specs=[VMEM, VMEM, HBM, HBM],
        out_shape=[
            jax.ShapeDtypeStruct((sources, capacity, width), BF16),
            jax.ShapeDtypeStruct((owned, width), F32),
        ],
        scratch_shapes=[
            pltpu.VMEM(gate_up.shape, BF16),
            pltpu.VMEM(down.shape, BF16),
            pltpu.SemaphoreType.DMA((chunks + 1,)),
        ],
        compiler_params=pltpu.CompilerParams(vmem_limit_bytes=24 << 20),
        name="run_expert",
    )(parts, gain.reshape(1, width), in_hbm(gate_up), in_hbm(down))


def weigh(returned, lists, weights, place, sizes):
    n_ctx, n_head, n_pair, rows_own, top, capacity = sizes
    slots, width = n_ctx * capacity, returned.shape[2]
    rows = lists.shape[1]

    def kernel(place_ref, x_ref, l_ref, g_ref, o_ref):
        slot = iota((slots, rows), 0)
        expert = slot // capacity * n_head * n_pair + place_ref[0] * n_pair + place_ref[1]
        hits = jnp.zeros((slots, rows), F32)
        factor = jnp.zeros((slots, rows), F32)
        for k in range(top):
            same = l_ref[k : k + 1, :] == expert
            hits = jnp.where(same, 1.0, hits)
            factor = jnp.where(same, g_ref[k : k + 1, :], factor)
        earlier = (iota((rows, rows), 0) < iota((rows, rows), 1)).astype(F32).astype(BF16)
        rank = dot(hits.astype(BF16), earlier)
        factor = jnp.where(rank == (slot % capacity).astype(F32), factor, 0.0)
        x = x_ref[...].reshape(slots, width)
        out = jnp.zeros((rows, width), F32)
        for piece in pieces(factor):
            out = out + lax.dot_general(
                piece.astype(BF16), x, (((0,), (0,)), ((), ())), preferred_element_type=F32
            )
        o_ref[...] = out.reshape(n_head * n_pair, rows_own, width)

    return pl.pallas_call(
        kernel,
        in_specs=[SMEM, VMEM, VMEM, VMEM],
        out_shape=jax.ShapeDtypeStruct((n_head * n_pair, rows_own, width), F32),
        compiler_params=pltpu.CompilerParams(vmem_limit_bytes=LIMIT),
        name="weigh",
    )(place, returned, lists, weights)


def finish(own, shares):
    rows_own = shares.shape[1]

    def kernel(h_ref, x_ref, o_ref):
        o_ref[...] = (h_ref[0:rows_own, :] + jnp.sum(x_ref[...], axis=0)).astype(BF16)

    return pl.pallas_call(
        kernel,
        out_shape=jax.ShapeDtypeStruct(shares.shape[1:], BF16),
        compiler_params=pltpu.CompilerParams(vmem_limit_bytes=LIMIT),
        name="finish",
    )(own, shares)


def body(
    queries,
    prompt_keys,
    prompt_values,
    residual,
    out_weight,
    norm_gain,
    expert_lists,
    gate_weights,
    gate_up,
    down_proj,
):
    n_ctx = lax.axis_size("ctx")
    n_head = lax.axis_size("head")
    n_pair = lax.axis_size("pair")
    rows_own, width = residual.shape
    rows_all, heads, head_size = queries.shape
    block_rows, top = expert_lists.shape
    capacity = 2
    rows_half = n_head * rows_own
    pairs_block = rows_half * heads
    sizes = (n_ctx, n_head, n_pair, rows_own, top, capacity)
    head, pair = lax.axis_index("head"), lax.axis_index("pair")
    place = jnp.stack([head, pair]).astype(jnp.int32)

    units = queries.reshape(n_ctx * n_head, n_pair, rows_own * heads, head_size)
    keys = prompt_keys.reshape(-1, head_size)
    values = prompt_values.reshape(-1, head_size)
    theirs = attend_half((1 - pair).reshape(1), units, keys, values, n_ctx, pairs_block)
    swapped = lax.ppermute(theirs, "pair", [(0, 1), (1, 0)])
    ours = attend_half(pair.reshape(1), units, keys, values, n_ctx, pairs_block)
    lists, weights = expert_lists.T, gate_weights.T
    merged = merge_pair(ours, swapped, residual, lists)
    parts = lax.all_to_all(merged, "ctx", 0, 0, tiled=True)
    copies = combine_all(parts, rows_half, heads)
    picks, owns, weight_here = selection(parts, place, sizes, (out_weight,))
    attended = lax.all_to_all(copies, "ctx", 0, 0, tiled=True)
    attended, picks, owns = lax.optimization_barrier((attended, picks, owns))
    partial = project(attended, weight_here, parts, place, rows_half, heads, n_head * n_pair)
    partials = lax.all_to_all(partial, ("head", "pair"), 0, 0, tiled=True)
    sending = dispatch(partials, picks, owns, n_ctx, n_head, n_pair)
    arrived = lax.all_to_all(sending, "ctx", 0, 0, tiled=True)
    produced, own = run_expert(arrived, norm_gain, gate_up[0], down_proj[0], capacity)
    returned = lax.all_to_all(produced, "ctx", 0, 0, tiled=True)
    weighted = weigh(returned, lists, weights, place, sizes)
    shares = lax.all_to_all(weighted, ("head", "pair"), 0, 0, tiled=True)
    return finish(own, shares)


def solution(mesh):
    in_specs = (
        P("groups", "head", None),
        P(("groups", "ctx", "pair"), "head", None),
        P(("groups", "ctx", "pair"), "head", None),
        P(("groups", "ctx", "head", "pair"), None),
        P("head", "ctx"),
        P(),
        P(("groups", "ctx"), None),
        P(("groups", "ctx"), None),
        P(("ctx", "head", "pair"), None, None),
        P(("ctx", "head", "pair"), None, None),
    )
    out_specs = P(("groups", "ctx", "head", "pair"), None)
    return jax.shard_map(body, mesh=mesh, in_specs=in_specs, out_specs=out_specs, check_vma=False)
```

time: 172 us -> 150 us (0.87)
  blocking collectives: 48.5 us -> 83.3 us
  starting transfers between devices: 49.6 us -> 32 us
  waiting for transfers between devices: 27.1 us -> 12 us
  local copies, waits for them, and re-layouts: 13 us -> 0.02 us
  matrix products: 4.62 us -> 0 us
  other arithmetic: 2.79 us -> 0.08 us
  Pallas kernels: 25.2 us -> 22.5 us
    all_to_all x1 -> x3, blocking collectives: 11.5 us -> 46.8 us  [the longest x1 19.1 us: body(): returned = lax.all_to_all(produced, 'ctx', 0, 0, tiled=True)]
    all_to_all x2 -> x0, starting transfers between devices: 17.6 us -> none  [the longest x1 10.1 us: body(): partials = lax.all_to_all(partial, ('head', 'pair'), 0, 0, tiled=True)]
    all_to_all x2 -> x0, waiting for transfers between devices: 14.1 us -> none  [the longest x1 10.4 us: body(): lax.all_to_all(produced.reshape(n_ctx, capacity, width), 'ctx', 0, 0, til...]
    unnamed x26 -> x6, local copies, waits for them, and re-layouts: 9.84 us -> 0.02 us
    dot_general x2 -> x0, matrix products: 4.62 us -> none  [the longest x1 4 us: body(): both = jnp.dot(normed, gate_up[0], preferred_element_type=F32)]
    reshape x4 -> x0, local copies, waits for them, and re-layouts: 3.12 us -> none  [the longest x1 0.98 us: body(): weighted.reshape(n_head * n_pair, rows_own, width)]
    convert_element_type x2 -> x0, other arithmetic: 2.14 us -> none  [the longest x1 1.45 us: body(): return (own[:rows_own] + jnp.sum(shares, axis=0)).astype(BF16)]
    pallas_call x8 -> x9, Pallas kernels: 23.3 us -> 22.2 us  [the longest x2 11.9 us: attend_half(): pl.pallas_call(kernel, in_specs=[SMEM, HBM, HBM, HBM], out_specs=VMEM, ou...]
  transfers between devices with their start and end apart: 4 -> 2, of which waited for: 3 -> 1; matrix products, arithmetic and copies ran while one was open for 2% -> 0% of each run, Pallas kernels for 4% -> 5%
where the time goes in v2:
time: 150 us
  blocking collectives  83.3 us (56%)
  starting transfers between devices  32 us (21%)
  Pallas kernels  22.5 us (15%)
  waiting for transfers between devices  12 us (8%)
    ppermute x1, starting transfers between devices, body(): swapped = lax.ppermute(theirs, 'pair', [(0, 1), (1, 0)])  20.5 us
    all_to_all x1, blocking collectives, body(): returned = lax.all_to_all(produced, 'ctx', 0, 0, tiled=True)  19.1 us
    all_to_all x1, blocking collectives, body(): parts = lax.all_to_all(merged, 'ctx', 0, 0, tiled=True)  18.8 us
    all_to_all x1, blocking collectives, body(): arrived = lax.all_to_all(sending, 'ctx', 0, 0, tiled=True)  17.6 us
    all_to_all x1, blocking collectives, body(): partials = lax.all_to_all(partial, ('head', 'pair'), 0, 0, tiled=True)  16.2 us
    all_to_all x1, waiting for transfers between devices, body(): attended = lax.all_to_all(copies, 'ctx', 0, 0, tiled=True)  12 us
    pallas_call x2, Pallas kernels, attend_half(): pl.pallas_call(kernel, in_specs=[SMEM, HBM, HBM, HBM], out_specs=VMEM, ou...  11.9 us
    all_to_all x1, blocking collectives, body(): shares = lax.all_to_all(weighted, ('head', 'pair'), 0, 0, tiled=True)  11.5 us
  transfers between devices with their start and end apart: 2, of which 1 were waited for; matrix products, arithmetic and copies ran while one was open for 0% of the time, Pallas kernels for 5%

profile of v2, /device:TPU:33, one launch (start us, length us, event | category | flops | bytes accessed | tf_op | source)
XLA Modules:
  0.0 149.9 jit_solution(3284886215151056203)
XLA Ops:
  0.0 0.0 copy-start.1
  0.0 5.9 %attend.3 = bf16[16,72,128]{2,1,0:T(8,128)(2,1)S(1)} custom-call(s32[1]{0:T(128)} %bitcast.5.half_ref, bf16[64,2,16,128]{3,2,1,0:T(8,128)(2,1)} %bitcast.17, bf16[2048,128]{1,0:T(8,128)(2,1)} %bitcast.19, bf16[2048,128]{1,0:T(8,128)(2,1)} %bitcast.21), custom_call_target="tpu_custom_call" | custom-call | tf_op jit(solution)/shard_map/attend/pallas_call | solution.py:98
  6.0 20.5 %collective-permute-start = (bf16[16,72,128]{2,1,0:T(8,128)(2,1)S(1)}, bf16[16,72,128]{2,1,0:T(8,128)(2,1)S(1)}, u32[]{:S(2)}, u32[]{:S(2)}) collective-permute-start(bf16[16,72,128]{2,1,0:T(8,128)(2,1)S(1)} %attend.3), channel_id=1, source_target_pairs={{0,1},{1,0},{2,3},{3,2},{4,5},{5,4},{6,7},{7,6},{8,9},{9,8},{10,11... | collective-permute-start | bytes 884744 | tf_op jit(solution)/shard_map/ppermute | solution.py:443
  26.5 5.9 %attend.2.a_ref = bf16[16,72,128]{2,1,0:T(8,128)(2,1)S(1)} custom-call(s32[1]{0:T(128)} %bitcast.1.half_ref, bf16[64,2,16,128]{3,2,1,0:T(8,128)(2,1)} %bitcast.18, bf16[2048,128]{1,0:T(8,128)(2,1)} %bitcast.20, bf16[2048,128]{1,0:T(8,128)(2,1)} %bitcast.22), custom_call_target="tpu_custom_call" | custom-call | tf_op jit(solution)/shard_map/attend/pallas_call | solution.py:98
  32.4 0.0 collective-permute-done.b_ref
  32.4 0.9 merge_pair.1
  33.3 18.8 %all_to_all.30.x_ref.s_ref = bf16[16,72,128]{2,1,0:T(8,128)(2,1)S(1)} all-to-all(bf16[16,72,128]{2,1,0:T(8,128)(2,1)S(1)} %merge_pair.1), channel_id=1, replica_groups=mesh['groups'=2,'ctx'=16,'head'=4,'pair'=2] {'ctx'}, dimensions={0} | all-to-all | bytes 589824 | tf_op jit(solution)/shard_map/all_to_all | solution.py:447
  52.1 1.1 combine_all.1
  53.2 11.4 %all-to-all-start.1 = ((bf16[16,64,128]{2,1,0:T(8,128)(2,1)}), bf16[16,64,128]{2,1,0:T(8,128)(2,1)S(1)}, u32[]{:S(2)}, u32[]{:S(2)}) async-start(bf16[16,64,128]{2,1,0:T(8,128)(2,1)} %combine_all.1), calls=%async_computation.1 | async-start | bytes 524288 | tf_op jit(solution)/shard_map/all_to_all | solution.py:450
  64.7 0.1 pad_add_fusion.place_ref
  64.8 1.5 %selection.1 = (bf16[512,256]{1,0:T(8,128)(2,1)S(1)}, bf16[128,256]{1,0:T(8,128)(2,1)S(1)}, bf16[1024,128]{1,0:T(8,128)(2,1)S(1)}) custom-call(s32[2]{0:T(128)S(1)} %pad_add_fusion.place_ref, bf16[16,72,128]{2,1,0:T(8,128)(2,1)S(1)} %all_to_all.30.x_ref.s_ref, bf16[1024,128]{1,0:T(8,128)(2,1)} %refs_0_.1), custom_call_target="tpu_custom_call" | custom-call | tf_op jit(solution)/shard_map/selection/pallas_call | solution.py:278
  66.3 0.0 copy-start
  66.3 0.0 copy-start.2
  66.3 12.0 %all-to-all-done.1.a_ref = bf16[16,64,128]{2,1,0:T(8,128)(2,1)S(1)} async-done(((bf16[16,64,128]{2,1,0:T(8,128)(2,1)}), bf16[16,64,128]{2,1,0:T(8,128)(2,1)S(1)}, u32[]{:S(2)}, u32[]{:S(2)}) %all-to-all-start.1) | async-done | bytes 262176 | tf_op jit(solution)/shard_map/all_to_all | solution.py:450
  78.3 0.8 project.1
  79.1 16.2 %all_to_all.31.x_ref = bf16[8,128,128]{2,1,0:T(8,128)(2,1)S(1)} all-to-all(bf16[8,128,128]{2,1,0:T(8,128)(2,1)S(1)} %project.1), channel_id=1, replica_groups=mesh['groups'=2,'ctx'=16,'head'=4,'pair'=2] {'head','pair'}, dimensions={0} | all-to-all | bytes 524288 | tf_op jit(solution)/shard_map/all_to_all | solution.py:453
  95.3 0.2 dispatch.1
  95.5 17.6 %all_to_all.32.x_ref = bf16[16,40,128]{2,1,0:T(8,128)(2,1)S(1)} all-to-all(bf16[16,40,128]{2,1,0:T(8,128)(2,1)S(1)} %dispatch.1), channel_id=1, replica_groups=mesh['groups'=2,'ctx'=16,'head'=4,'pair'=2] {'ctx'}, dimensions={0} | all-to-all | bytes 327680 | tf_op jit(solution)/shard_map/all_to_all | solution.py:455
  113.1 0.0 copy-done.1
  113.1 4.5 %run_expert.1 = (bf16[16,2,2048]{2,1,0:T(2,128)(2,1)S(1)}, f32[8,2048]{1,0:T(8,128)S(1)}) custom-call(bf16[16,40,128]{2,1,0:T(8,128)(2,1)S(1)} %all_to_all.32.x_ref, f32[1,2048]{1,0:T(1,128)S(1)} %bitcast.13, bf16[2048,1536]{1,0:T(8,128)(2,1)} %bitcast.15, bf16[768,2048]{1,0:T(8,128)(2,1)} %bitcast.16), custom_call_target="tpu_custom_call" | custom-call | tf_op jit(solution)/shard_map/run_expert/pallas_call | solution.py:349
  117.7 19.1 %all_to_all.33.x_ref = bf16[16,2,2048]{2,1,0:T(2,128)(2,1)S(1)} all-to-all(bf16[16,2,2048]{2,1,0:T(2,128)(2,1)S(1)} %get-tuple-element.20), channel_id=1, replica_groups=mesh['groups'=2,'ctx'=16,'head'=4,'pair'=2] {'ctx'}, dimensions={0} | all-to-all | bytes 262144 | tf_op jit(solution)/shard_map/all_to_all | solution.py:457
  136.8 0.0 copy-done
  136.8 0.0 copy-done.2
  136.8 0.9 weigh.1
  137.8 11.5 %all_to_all.34.x_ref = f32[8,2,2048]{2,1,0:T(2,128)S(1)} all-to-all(f32[8,2,2048]{2,1,0:T(2,128)S(1)} %weigh.1), channel_id=1, replica_groups=mesh['groups'=2,'ctx'=16,'head'=4,'pair'=2] {'head','pair'}, dimensions={0} | all-to-all | bytes 262144 | tf_op jit(solution)/shard_map/all_to_all | solution.py:459
  149.2 0.7 finish.1
Async XLA Ops:
  0.0 113.1 %copy-start.1 = (f32[2048]{0:T(1024)S(1)}, f32[2048]{0:T(1024)}, u32[]{:S(2)}) copy-start(f32[2048]{0:T(1024)} %param.15) | copy-start | bytes 24580
  6.0 26.5 %collective-permute-start = (bf16[16,72,128]{2,1,0:T(8,128)(2,1)S(1)}, bf16[16,72,128]{2,1,0:T(8,128)(2,1)S(1)}, u32[]{:S(2)}, u32[]{:S(2)}) collective-permute-start(bf16[16,72,128]{2,1,0:T(8,128)(2,1)S(1)} %attend.3), channel_id=1, source_target_pairs={{0,1},{1,0},{2,3},{3,2},{4,5},{5,4},{6,7},{7,6},{8,9},{9,8},{10,11... | collective-permute-start | bytes 884744 | tf_op jit(solution)/shard_map/ppermute | solution.py:443
  53.2 25.1 %all-to-all-start.1 = ((bf16[16,64,128]{2,1,0:T(8,128)(2,1)}), bf16[16,64,128]{2,1,0:T(8,128)(2,1)S(1)}, u32[]{:S(2)}, u32[]{:S(2)}) async-start(bf16[16,64,128]{2,1,0:T(8,128)(2,1)} %combine_all.1), calls=%async_computation.1 | async-start | bytes 524288 | tf_op jit(solution)/shard_map/all_to_all | solution.py:450
  66.3 70.5 %copy-start = (s32[16,8]{0,1:T(8,128)S(1)}, s32[16,8]{0,1:T(8,128)}, u32[]{:S(2)}) copy-start(s32[16,8]{0,1:T(8,128)} %param.16) | copy-start | bytes 1540
  66.3 70.5 %copy-start.2 = (f32[16,8]{0,1:T(8,128)S(1)}, f32[16,8]{0,1:T(8,128)}, u32[]{:S(2)}) copy-start(f32[16,8]{0,1:T(8,128)} %param.17) | copy-start | bytes 1540

commit v3 on v2

v3 whole, which is shorter than its diff:
```python
import math

import jax
import jax.numpy as jnp
from jax import lax
from jax.experimental import pallas as pl
from jax.experimental.pallas import tpu as pltpu
from jax.sharding import PartitionSpec as P

F32 = jnp.float32
BF16 = jnp.bfloat16
LIMIT = 16 << 20
LOG2E = math.log2(math.e)
STATS = 8


SMEM = pl.BlockSpec(memory_space=pltpu.SMEM)
VMEM = pl.BlockSpec(memory_space=pltpu.VMEM)
HBM = pl.BlockSpec(memory_space=pltpu.HBM)


def in_hbm(x):
    return pltpu.with_memory_space_constraint(x, pltpu.HBM)


def iota(shape, dim):
    return lax.broadcasted_iota(jnp.int32, shape, dim)


def dot(a, b):
    return lax.dot_general(a, b, (((1,), (0,)), ((), ())), preferred_element_type=F32)


def as_row(column, lanes):
    n = column.shape[0]
    here = iota((n, lanes), 0) == iota((n, lanes), 1)
    return jnp.sum(jnp.where(here, jnp.broadcast_to(column, (n, lanes)), 0.0), axis=0, keepdims=True)


def as_column(row, n):
    lanes = row.shape[1]
    here = iota((n, lanes), 0) == iota((n, lanes), 1)
    return jnp.sum(jnp.where(here, jnp.broadcast_to(row, (n, lanes)), 0.0), axis=1, keepdims=True)


def pieces(row):
    first = row.astype(BF16).astype(F32)
    second = (row - first).astype(BF16).astype(F32)
    third = row - first - second
    return first, second, third


def stacked(rows, lanes):
    at = iota((STATS, lanes), 0)
    out = jnp.zeros((STATS, lanes), F32)
    for i, row in enumerate(rows):
        out = jnp.where(at == i, jnp.broadcast_to(row, (STATS, lanes)), out)
    return out


def attend_tiles(q_ref, k_ref, v_ref, o_ref, score_refs, tile_units, tile_blocks, pairs_block, ready):
    units, unit, width = q_ref.shape
    tile = tile_units * unit
    steps = units // tile_units
    scale = LOG2E / math.sqrt(width)

    def scores(i):
        q = q_ref[i * tile_units : (i + 1) * tile_units].reshape(tile, width)
        score_refs[i % 2][...] = lax.dot_general(
            q, k_ref[...], (((1,), (1,)), ((), ())), preferred_element_type=F32
        )

    scores(0)
    ready()
    for i in range(steps):
        if i + 1 < steps:
            scores(i + 1)
        here = score_refs[i % 2][...]
        top = jnp.max(here, axis=1, keepdims=True)
        probs = jnp.exp2((here - top) * scale)
        total = jnp.sum(probs, axis=1, keepdims=True)
        out = dot(probs.astype(BF16), v_ref[...]) / total
        level = top * scale + jnp.log(total) * LOG2E
        for b in range(tile_blocks):
            part = slice(b * pairs_block, (b + 1) * pairs_block)
            at = i * tile_blocks + b
            o_ref[at, 0:pairs_block, :] = out[part].astype(BF16)
            row = as_row(level[part], width)
            o_ref[at, pairs_block : pairs_block + STATS, :] = stacked(pieces(row), width).astype(BF16)


def attend(pair, queries, keys, values, blocks, pairs_block):
    units, _, unit, width = queries.shape
    length = keys.shape[0]
    tile_blocks = max(1, 256 // pairs_block)
    tile_units = tile_blocks * units // blocks
    out_shape = jax.ShapeDtypeStruct((blocks, pairs_block + STATS, width), BF16)
    scores = [pltpu.VMEM((tile_units * unit, length), F32)] * 2
    params = pltpu.CompilerParams(vmem_limit_bytes=24 << 20)

    def first(pair_ref, q_hbm, k_hbm, v_hbm, o_ref, q_own, k_ref, v_ref, q_ref, score_a, score_b, sems):
        copy_k = pltpu.make_async_copy(k_hbm, k_ref, sems.at[0])
        copy_q = pltpu.make_async_copy(q_hbm.at[:, 1 - pair_ref[0]], q_ref, sems.at[1])
        copy_v = pltpu.make_async_copy(v_hbm, v_ref, sems.at[2])
        copy_own = pltpu.make_async_copy(q_hbm.at[:, pair_ref[0]], q_own, sems.at[3])
        copy_q.start()
        copy_k.start()
        copy_v.start()
        copy_own.start()
        copy_q.wait()
        copy_k.wait()
        attend_tiles(
            q_ref, k_ref, v_ref, o_ref, (score_a, score_b), tile_units, tile_blocks, pairs_block, copy_v.wait
        )
        copy_own.wait()

    def second(q_ref, k_ref, v_ref, o_ref, score_a, score_b):
        attend_tiles(
            q_ref, k_ref, v_ref, o_ref, (score_a, score_b), tile_units, tile_blocks, pairs_block, lambda: None
        )

    theirs, q_own, k_here, v_here = pl.pallas_call(
        first,
        in_specs=[SMEM, HBM, HBM, HBM],
        out_specs=[VMEM] * 4,
        out_shape=[
            out_shape,
            jax.ShapeDtypeStruct((units, unit, width), BF16),
            jax.ShapeDtypeStruct(keys.shape, BF16),
            jax.ShapeDtypeStruct(values.shape, BF16),
        ],
        scratch_shapes=[pltpu.VMEM((units, unit, width), BF16), *scores, pltpu.SemaphoreType.DMA((4,))],
        compiler_params=params,
        name="attend_theirs",
    )(pair.reshape(1), in_hbm(queries), in_hbm(keys), in_hbm(values))
    swapped = lax.ppermute(theirs, "pair", [(0, 1), (1, 0)])
    ours = pl.pallas_call(
        second,
        in_specs=[VMEM] * 3,
        out_specs=VMEM,
        out_shape=out_shape,
        scratch_shapes=scores,
        compiler_params=params,
        name="attend_ours",
    )(q_own, k_here, v_here)
    return ours, swapped


def levels_of(ref, pairs_block):
    stats = ref[:, pairs_block : pairs_block + STATS, :].astype(F32)
    return stats[:, 0, :] + stats[:, 1, :] + stats[:, 2, :]


def merge_pair(mine, other, residual, names, weights):
    blocks, height, width = mine.shape
    pairs_block = height - STATS

    def kernel(a_ref, b_ref, r_hbm, n_hbm, g_hbm, o_ref, r_ref, n_ref, g_ref, sems):
        copy_r = pltpu.make_async_copy(r_hbm, r_ref, sems.at[0])
        copy_n = pltpu.make_async_copy(n_hbm, n_ref, sems.at[1])
        copy_g = pltpu.make_async_copy(g_hbm, g_ref, sems.at[2])
        copy_r.start()
        copy_n.start()
        copy_g.start()
        level_a, level_b = levels_of(a_ref, pairs_block), levels_of(b_ref, pairs_block)
        highest = jnp.maximum(level_a, level_b)
        share_a, share_b = jnp.exp2(level_a - highest), jnp.exp2(level_b - highest)
        total = share_a + share_b
        share_a, share_b = share_a / total, share_b / total
        level = highest + jnp.log(total) * LOG2E
        first, second, third = pieces(level)
        for b in range(blocks):
            col_a, col_b = as_column(share_a[b : b + 1], pairs_block), as_column(share_b[b : b + 1], pairs_block)
            both = a_ref[b, 0:pairs_block, :].astype(F32) * col_a + b_ref[b, 0:pairs_block, :].astype(F32) * col_b
            o_ref[b, 0:pairs_block, :] = both.astype(BF16)
        copy_r.wait()
        copy_n.wait()
        copy_g.wait()
        residual_all = r_ref[...].astype(F32)
        top, rows = n_ref.shape
        spread = (iota((rows, width), 1) % rows == iota((rows, width), 0)).astype(F32).astype(BF16)
        kept = iota((top, width), 1) // rows == iota((top, width), 0)

        def in_lanes(table):
            return jnp.sum(jnp.where(kept, dot(table.astype(BF16), spread), 0.0), axis=0, keepdims=True)

        listed = in_lanes(n_ref[...].astype(F32))
        gates = g_ref[...]
        rounded = gates.astype(BF16).astype(F32)
        gate_first, gate_second = in_lanes(rounded), in_lanes(gates - rounded)
        for b in range(blocks):
            own = residual_all[:, b * width : (b + 1) * width]
            rows_b = (first[b : b + 1], second[b : b + 1], third[b : b + 1], own[0:1], own[1:2], listed)
            rows_b = rows_b + (gate_first, gate_second)
            o_ref[b, pairs_block:height, :] = stacked(rows_b, width).astype(BF16)

    return pl.pallas_call(
        kernel,
        in_specs=[VMEM, VMEM, HBM, HBM, HBM],
        out_shape=jax.ShapeDtypeStruct((blocks, height, width), BF16),
        scratch_shapes=[
            pltpu.VMEM(residual.shape, residual.dtype),
            pltpu.VMEM(names.shape, names.dtype),
            pltpu.VMEM(weights.shape, weights.dtype),
            pltpu.SemaphoreType.DMA((3,)),
        ],
        compiler_params=pltpu.CompilerParams(vmem_limit_bytes=LIMIT),
        name="merge_pair",
    )(mine, other, in_hbm(residual), in_hbm(names), in_hbm(weights))


def combine_all(parts, rows_half, heads):
    sources, height, width = parts.shape
    pairs_block = height - STATS

    def kernel(x_ref, o_hbm, acc_ref, att_ref, sem):
        level = levels_of(x_ref, pairs_block)
        share = jnp.exp2(level - jnp.max(level, axis=0, keepdims=True))
        share = share / jnp.sum(share, axis=0, keepdims=True)
        acc = jnp.zeros((pairs_block, width), F32)
        for s in range(sources):
            acc = acc + x_ref[s, 0:pairs_block, :].astype(F32) * as_column(share[s : s + 1], pairs_block)
        acc_ref[...] = acc
        by_head = [acc_ref[pl.ds(h, rows_half, stride=heads), :] for h in range(heads)]
        att_ref[...] = jnp.concatenate(by_head, axis=0).astype(BF16)
        copies = [pltpu.make_async_copy(att_ref, o_hbm.at[s], sem.at[s]) for s in range(sources)]
        for copy in copies:
            copy.start()
        for copy in copies:
            copy.wait()

    return pl.pallas_call(
        kernel,
        in_specs=[VMEM],
        out_specs=HBM,
        out_shape=pltpu.HBM((sources, pairs_block, width), BF16),
        scratch_shapes=[
            pltpu.VMEM((pairs_block, width), F32),
            pltpu.VMEM((pairs_block, width), BF16),
            pltpu.SemaphoreType.DMA((sources,)),
        ],
        compiler_params=pltpu.CompilerParams(vmem_limit_bytes=LIMIT),
        name="combine_all",
    )(parts)


def project(attended, weight, parts, place, rows_half, heads, copies):
    blocks, pairs_block, width = attended.shape
    columns = weight.shape[1]
    rows = blocks * rows_half

    def kernel(place_ref, a_ref, w_ref, s_ref, o_ref):
        a = a_ref[...].astype(F32)
        by_head = [a[:, h * rows_half : (h + 1) * rows_half, :].reshape(rows, width) for h in range(heads)]
        out = dot(jnp.concatenate(by_head, axis=1).astype(BF16), w_ref[...])
        out = out.reshape(blocks, rows_half, columns)
        stats = s_ref[:, pairs_block : pairs_block + STATS, :].astype(F32)
        at = iota((blocks, rows_half, columns), 1)
        first = 2 * place_ref[0]
        out = out + jnp.where(at == first, stats[:, 3:4, :], 0.0) + jnp.where(at == first + 1, stats[:, 4:5, :], 0.0)
        out = out.reshape(rows, columns).astype(BF16)
        for i in range(copies):
            o_ref[i] = out

    return pl.pallas_call(
        kernel,
        in_specs=[SMEM, VMEM, VMEM, VMEM],
        out_shape=jax.ShapeDtypeStruct((copies, rows, columns), BF16),
        compiler_params=pltpu.CompilerParams(vmem_limit_bytes=LIMIT),
        name="project",
    )(place, attended, weight, parts)


def selection(parts, place, sizes, fetched):
    n_ctx, n_head, n_pair, rows_own, top, capacity = sizes
    block_rows = n_head * n_pair * rows_own
    rows_all = n_ctx * block_rows
    blocks, height, width = parts.shape
    per_peer = n_ctx * capacity

    def natural(lane):
        pair = lane // (rows_all // n_pair)
        rest = lane % (rows_all // n_pair)
        block = rest // (n_head * rows_own)
        head = (rest // rows_own) % n_head
        return block, (head * n_pair + pair) * rows_own + rest % rows_own

    count_fetched = len(fetched)

    def kernel(place_ref, s_ref, *refs):
        sources, d_ref, o_ref = refs[:count_fetched], refs[count_fetched], refs[count_fetched + 1]
        targets, sems = refs[count_fetched + 2 : -1], refs[-1]
        fetches = [pltpu.make_async_copy(a, b, sems.at[i]) for i, (a, b) in enumerate(zip(sources, targets))]
        for fetch in fetches:
            fetch.start()
        stats = s_ref[:, height - STATS : height, :].astype(F32)
        listed = stats[:, 5, :]
        count = n_ctx * n_ctx
        repeated = jnp.concatenate([listed] * n_ctx, axis=0)
        expert = (iota((count, width), 0) // n_ctx * n_head * n_pair + place_ref[0] * n_pair + place_ref[1]).astype(F32)
        equal = (repeated == expert).astype(F32).astype(BF16)
        fold = (iota((width, block_rows), 0) % block_rows == iota((width, block_rows), 1)).astype(F32).astype(BF16)
        hits = dot(equal, fold)
        earlier = (iota((block_rows, block_rows), 0) < iota((block_rows, block_rows), 1)).astype(F32).astype(BF16)
        rank = dot(hits.astype(BF16), earlier)
        slot = jnp.where(hits > 0.5, rank + 1.0, 0.0).astype(BF16)
        expand = iota((count * capacity, count), 0) // capacity == iota((count * capacity, count), 1)
        slot = dot(expand.astype(F32).astype(BF16), slot).astype(BF16)
        block, row = natural(iota((block_rows, rows_all), 1))
        spread = (iota((block_rows, rows_all), 0) == row).astype(F32).astype(BF16)
        slot = dot(slot, spread)
        at = iota((count * capacity, rows_all), 0)
        block, row = natural(iota((count * capacity, rows_all), 1))
        mine = (block == (at // capacity) % n_ctx) & (slot == (at % capacity + 1).astype(F32))
        d_ref[...] = mine.astype(F32).astype(BF16)
        own = (place_ref[2] * n_head * n_pair + place_ref[0] * n_pair + place_ref[1]).astype(F32)
        same = (listed == own).astype(F32).astype(BF16)
        rank = dot(dot(same, fold).astype(BF16), earlier).astype(BF16)
        back = (iota((block_rows, width), 1) % block_rows == iota((block_rows, width), 0)).astype(F32).astype(BF16)
        twice = iota((per_peer, n_ctx), 0) // capacity == iota((per_peer, n_ctx), 1)
        twice = twice.astype(F32).astype(BF16)
        rank = dot(twice, dot(rank, back).astype(BF16))
        used = (dot(twice, same) > 0.5) & (rank == (iota((per_peer, width), 0) % capacity).astype(F32))
        gates = dot(twice, stats[:, 6, :].astype(BF16)) + dot(twice, stats[:, 7, :].astype(BF16))
        gate = jnp.sum(jnp.where(used, gates, 0.0), axis=1, keepdims=True)
        is_first = used & (iota((per_peer, width), 1) < block_rows)
        is_first = jnp.sum(jnp.where(is_first, 1.0, 0.0), axis=1, keepdims=True)
        o_ref[...] = jnp.where(iota((per_peer, width), 1) == 0, gate, is_first)
        for fetch in fetches:
            fetch.wait()

    return pl.pallas_call(
        kernel,
        in_specs=[SMEM, VMEM] + [HBM] * count_fetched,
        out_specs=[VMEM] * (2 + count_fetched),
        out_shape=[
            jax.ShapeDtypeStruct((n_ctx * per_peer, rows_all), BF16),
            jax.ShapeDtypeStruct((per_peer, width), F32),
        ]
        + [jax.ShapeDtypeStruct(x.shape, x.dtype) for x in fetched],
        scratch_shapes=[pltpu.SemaphoreType.DMA((count_fetched,))],
        compiler_params=pltpu.CompilerParams(vmem_limit_bytes=LIMIT),
        name="selection",
    )(place, parts, *[in_hbm(x) for x in fetched])


def dispatch(partials, picks, n_ctx, n_head, n_pair):
    copies, rows, columns = partials.shape
    per_peer = picks.shape[0] // n_ctx

    def kernel(x_ref, d_ref, o_ref):
        halves = []
        for p in range(n_pair):
            acc = x_ref[p].astype(F32)
            for h in range(1, n_head):
                acc = acc + x_ref[h * n_pair + p].astype(F32)
            halves.append(acc)
        hidden = jnp.concatenate(halves, axis=0).astype(BF16)
        o_ref[...] = dot(d_ref[...], hidden).reshape(n_ctx, per_peer, columns).astype(BF16)

    return pl.pallas_call(
        kernel,
        out_shape=jax.ShapeDtypeStruct((n_ctx, per_peer, columns), BF16),
        compiler_params=pltpu.CompilerParams(vmem_limit_bytes=LIMIT),
        name="dispatch",
    )(partials, picks)


def run_expert(parts, slot_facts, gain, gate_up, down, capacity):
    sources, slots, columns = parts.shape
    width = sources * columns
    units = down.shape[0]
    chunks = 8
    chunk = width // chunks

    def kernel(x_ref, f_ref, g_ref, up_hbm, down_hbm, y_ref, up_ref, down_ref, sems):
        ups = [
            pltpu.make_async_copy(
                up_hbm.at[pl.ds(i * chunk, chunk)], up_ref.at[pl.ds(i * chunk, chunk)], sems.at[i]
            )
            for i in range(chunks)
        ]
        last = pltpu.make_async_copy(down_hbm, down_ref, sems.at[chunks])
        for copy in ups:
            copy.start()
        last.start()
        rows = jnp.concatenate([x_ref[s].astype(F32) for s in range(sources)], axis=1)
        mean = jnp.sum(rows * rows, axis=1, keepdims=True) * (1.0 / width)
        normed = (rows * lax.rsqrt(mean + 1e-06) * g_ref[...]).astype(BF16)
        both = jnp.zeros((slots, 2 * units), F32)
        for i in range(chunks):
            ups[i].wait()
            both = both + dot(normed[:, i * chunk : (i + 1) * chunk], up_ref[i * chunk : (i + 1) * chunk, :])
        gate = both[:, :units]
        inner = (gate / (1.0 + jnp.exp(-gate)) * both[:, units:]).astype(BF16)
        last.wait()
        out = dot(inner, down_ref[...]) * f_ref[:, 0:1] + rows * f_ref[:, 1:2]
        y_ref[...] = out.astype(BF16).reshape(sources, capacity, width)

    return pl.pallas_call(
        kernel,
        in_specs=[VMEM, VMEM, VMEM, HBM, HBM],
        out_shape=jax.ShapeDtypeStruct((sources, capacity, width), BF16),
        scratch_shapes=[
            pltpu.VMEM(gate_up.shape, BF16),
            pltpu.VMEM(down.shape, BF16),
            pltpu.SemaphoreType.DMA((chunks + 1,)),
        ],
        compiler_params=pltpu.CompilerParams(vmem_limit_bytes=24 << 20),
        name="run_expert",
    )(parts, slot_facts, gain.reshape(1, width), in_hbm(gate_up), in_hbm(down))


def sum_rows(returned, lists, place, sizes):
    n_ctx, n_head, n_pair, rows_own, top, capacity = sizes
    slots, width = n_ctx * capacity, returned.shape[2]
    rows = lists.shape[1]

    def kernel(place_ref, x_ref, l_ref, o_ref):
        slot = iota((slots, rows), 0)
        expert = slot // capacity * n_head * n_pair + place_ref[0] * n_pair + place_ref[1]
        hits = jnp.zeros((slots, rows), F32)
        for k in range(top):
            hits = jnp.where(l_ref[k : k + 1, :] == expert, 1.0, hits)
        earlier = (iota((rows, rows), 0) < iota((rows, rows), 1)).astype(F32).astype(BF16)
        rank = dot(hits.astype(BF16), earlier)
        taken = jnp.where(rank == (slot % capacity).astype(F32), hits, 0.0).astype(BF16)
        x = x_ref[...].reshape(slots, width)
        out = lax.dot_general(taken, x, (((0,), (0,)), ((), ())), preferred_element_type=F32)
        o_ref[...] = out.reshape(n_head * n_pair, rows_own, width)

    return pl.pallas_call(
        kernel,
        in_specs=[SMEM, VMEM, VMEM],
        out_shape=jax.ShapeDtypeStruct((n_head * n_pair, rows_own, width), F32),
        compiler_params=pltpu.CompilerParams(vmem_limit_bytes=LIMIT),
        name="sum_rows",
    )(place, returned, lists)


def finish(shares):
    def kernel(x_ref, o_ref):
        o_ref[...] = jnp.sum(x_ref[...], axis=0).astype(BF16)

    return pl.pallas_call(
        kernel,
        out_shape=jax.ShapeDtypeStruct(shares.shape[1:], BF16),
        compiler_params=pltpu.CompilerParams(vmem_limit_bytes=LIMIT),
        name="finish",
    )(shares)


def body(
    queries,
    prompt_keys,
    prompt_values,
    residual,
    out_weight,
    norm_gain,
    expert_lists,
    gate_weights,
    gate_up,
    down_proj,
):
    n_ctx = lax.axis_size("ctx")
    n_head = lax.axis_size("head")
    n_pair = lax.axis_size("pair")
    rows_own, width = residual.shape
    rows_all, heads, head_size = queries.shape
    block_rows, top = expert_lists.shape
    capacity = 2
    rows_half = n_head * rows_own
    pairs_block = rows_half * heads
    sizes = (n_ctx, n_head, n_pair, rows_own, top, capacity)
    head, pair = lax.axis_index("head"), lax.axis_index("pair")
    place = jnp.stack([head, pair, lax.axis_index("ctx")]).astype(jnp.int32)

    units = queries.reshape(n_ctx * n_head, n_pair, rows_own * heads, head_size)
    keys = prompt_keys.reshape(-1, head_size)
    values = prompt_values.reshape(-1, head_size)
    ours, swapped = attend(pair, units, keys, values, n_ctx, pairs_block)
    lists, weights = expert_lists.T, gate_weights.T
    merged = merge_pair(ours, swapped, residual, lists, weights)
    parts = lax.all_to_all(merged, "ctx", 0, 0, tiled=True)
    copies = combine_all(parts, rows_half, heads)
    picks, slot_facts, weight_here = selection(parts, place, sizes, (out_weight,))
    attended = lax.all_to_all(copies, "ctx", 0, 0, tiled=True)
    attended, picks, slot_facts = lax.optimization_barrier((attended, picks, slot_facts))
    partial = project(attended, weight_here, parts, place, rows_half, heads, n_head * n_pair)
    partials = lax.all_to_all(partial, ("head", "pair"), 0, 0, tiled=True)
    sending = dispatch(partials, picks, n_ctx, n_head, n_pair)
    arrived = lax.all_to_all(sending, "ctx", 0, 0, tiled=True)
    produced = run_expert(arrived, slot_facts, norm_gain, gate_up[0], down_proj[0], capacity)
    returned = lax.all_to_all(produced, "ctx", 0, 0, tiled=True)
    weighted = sum_rows(returned, lists, place, sizes)
    shares = lax.all_to_all(weighted, ("head", "pair"), 0, 0, tiled=True)
    return finish(shares)


def solution(mesh):
    in_specs = (
        P("groups", "head", None),
        P(("groups", "ctx", "pair"), "head", None),
        P(("groups", "ctx", "pair"), "head", None),
        P(("groups", "ctx", "head", "pair"), None),
        P("head", "ctx"),
        P(),
        P(("groups", "ctx"), None),
        P(("groups", "ctx"), None),
        P(("ctx", "head", "pair"), None, None),
        P(("ctx", "head", "pair"), None, None),
    )
    out_specs = P(("groups", "ctx", "head", "pair"), None)
    return jax.shard_map(body, mesh=mesh, in_specs=in_specs, out_specs=out_specs, check_vma=False)
```

time: 150 us -> 145 us (0.967)
  Pallas kernels: 22.5 us -> 18.4 us
  blocking collectives: 83.3 us -> 81.6 us
    pallas_call x6, Pallas kernels: 18.4 us -> 14.2 us  [the longest x1 4.55 us: run_expert(): pl.pallas_call(kernel, in_specs=[VMEM, VMEM, VMEM, HBM, HBM], out_shape=j...]
    all_to_all x1, blocking collectives: 19.1 us -> 17.5 us  [body(): returned = lax.all_to_all(produced, 'ctx', 0, 0, tiled=True)]
  transfers between devices with their start and end apart: 2 -> 2, of which waited for: 1 -> 1; matrix products, arithmetic and copies ran while one was open for 0% -> 0% of each run, Pallas kernels for 5% -> 3%
where the time goes in v3:
time: 145 us; the launch traced here: 144 us
  blocking collectives  81.6 us (56%)
  starting transfers between devices  32 us (22%)
  Pallas kernels  18.4 us (13%)
  waiting for transfers between devices  11.9 us (8%)
    ppermute x1, starting transfers between devices, attend(): swapped = lax.ppermute(theirs, 'pair', [(0, 1), (1, 0)])  20.5 us
    all_to_all x1, blocking collectives, body(): parts = lax.all_to_all(merged, 'ctx', 0, 0, tiled=True)  18.8 us
    all_to_all x1, blocking collectives, body(): returned = lax.all_to_all(produced, 'ctx', 0, 0, tiled=True)  17.5 us
    all_to_all x1, blocking collectives, body(): arrived = lax.all_to_all(sending, 'ctx', 0, 0, tiled=True)  17.4 us
    all_to_all x1, blocking collectives, body(): partials = lax.all_to_all(partial, ('head', 'pair'), 0, 0, tiled=True)  16.2 us
    all_to_all x1, waiting for transfers between devices, body(): attended = lax.all_to_all(copies, 'ctx', 0, 0, tiled=True)  11.8 us
    all_to_all x1, blocking collectives, body(): shares = lax.all_to_all(weighted, ('head', 'pair'), 0, 0, tiled=True)  11.7 us
    all_to_all x1, starting transfers between devices, body(): attended = lax.all_to_all(copies, 'ctx', 0, 0, tiled=True)  11.4 us
  transfers between devices with their start and end apart: 2, of which 1 were waited for; matrix products, arithmetic and copies ran while one was open for 0% of the time, Pallas kernels for 3%

profile of v3, /device:TPU:33, one launch (start us, length us, event | category | flops | bytes accessed | tf_op | source)
XLA Modules:
  0.0 144.0 jit_solution(2367172649978154188)
XLA Ops:
  0.0 0.0 copy-start.1
  0.0 4.5 %attend_theirs.1 = (bf16[16,72,128]{2,1,0:T(8,128)(2,1)S(1)}, bf16[64,16,128]{2,1,0:T(8,128)(2,1)S(1)}, bf16[2048,128]{1,0:T(8,128)(2,1)S(1)}, bf16[2048,128]{1,0:T(8,128)(2,1)S(1)}) custom-call(s32[1]{0:T(128)} %bitcast.1.pair_ref, bf16[64,2,16,128]{3,2,1,0:T(8,128)(2,1)} %bitcast.16, bf16[2048,128]{1,0:T(8,128)(2,1)} %bitcast.17, bf16[2048,128]{1,0:T(8,128)(2,1)} %bitcast.18), custom_call_target="tpu_custom_call" | custom-call | tf_op jit(solution)/shard_map/attend_theirs/pallas_call | solution.py:122
  4.5 20.5 %collective-permute-start = (bf16[16,72,128]{2,1,0:T(8,128)(2,1)S(1)}, bf16[16,72,128]{2,1,0:T(8,128)(2,1)S(1)}, u32[]{:S(2)}, u32[]{:S(2)}) collective-permute-start(bf16[16,72,128]{2,1,0:T(8,128)(2,1)S(1)} %get-tuple-element.18), channel_id=1, source_target_pairs={{0,1},{1,0},{2,3},{3,2},{4,5},{5,4},{6,7},{7,6},{8,9},{9,8},{10,11... | collective-permute-start | bytes 884744 | tf_op jit(solution)/shard_map/ppermute | solution.py:136
  25.1 3.2 %attend_ours.1.a_ref = bf16[16,72,128]{2,1,0:T(8,128)(2,1)S(1)} custom-call(bf16[64,16,128]{2,1,0:T(8,128)(2,1)S(1)} %get-tuple-element.15.q_ref, bf16[2048,128]{1,0:T(8,128)(2,1)S(1)} %get-tuple-element.16.k_ref, bf16[2048,128]{1,0:T(8,128)(2,1)S(1)} %get-tuple-element.17.v_ref), custom_call_target="tpu_custom_call" | custom-call | tf_op jit(solution)/shard_map/attend_ours/pallas_call | solution.py:137
  28.2 0.0 collective-permute-done.b_ref
  28.2 0.9 merge_pair.1
  29.1 18.8 %all_to_all.30.x_ref.s_ref = bf16[16,72,128]{2,1,0:T(8,128)(2,1)S(1)} all-to-all(bf16[16,72,128]{2,1,0:T(8,128)(2,1)S(1)} %merge_pair.1), channel_id=1, replica_groups=mesh['groups'=2,'ctx'=16,'head'=4,'pair'=2] {'ctx'}, dimensions={0} | all-to-all | bytes 589824 | tf_op jit(solution)/shard_map/all_to_all | solution.py:484
  48.0 1.1 combine_all.1
  49.1 11.4 %all-to-all-start.1 = ((bf16[16,64,128]{2,1,0:T(8,128)(2,1)}), bf16[16,64,128]{2,1,0:T(8,128)(2,1)S(1)}, u32[]{:S(2)}, u32[]{:S(2)}) async-start(bf16[16,64,128]{2,1,0:T(8,128)(2,1)} %combine_all.1), calls=%async_computation.1 | async-start | bytes 524288 | tf_op jit(solution)/shard_map/all_to_all | solution.py:487
  60.5 0.1 pad_add_fusion.place_ref
  60.6 1.7 %selection.1 = (bf16[512,256]{1,0:T(8,128)(2,1)S(1)}, f32[32,128]{1,0:T(8,128)S(1)}, bf16[1024,128]{1,0:T(8,128)(2,1)S(1)}) custom-call(s32[3]{0:T(128)S(1)} %pad_add_fusion.place_ref, bf16[16,72,128]{2,1,0:T(8,128)(2,1)S(1)} %all_to_all.30.x_ref.s_ref, bf16[1024,128]{1,0:T(8,128)(2,1)} %refs_0_.1), custom_call_target="tpu_custom_call" | custom-call | tf_op jit(solution)/shard_map/selection/pallas_call | solution.py:332
  62.3 0.0 copy-start
  62.3 11.8 %all-to-all-done.1.a_ref = bf16[16,64,128]{2,1,0:T(8,128)(2,1)S(1)} async-done(((bf16[16,64,128]{2,1,0:T(8,128)(2,1)}), bf16[16,64,128]{2,1,0:T(8,128)(2,1)S(1)}, u32[]{:S(2)}, u32[]{:S(2)}) %all-to-all-start.1) | async-done | bytes 262176 | tf_op jit(solution)/shard_map/all_to_all | solution.py:487
  74.1 0.8 project.1
  74.9 16.2 %all_to_all.31.x_ref = bf16[8,128,128]{2,1,0:T(8,128)(2,1)S(1)} all-to-all(bf16[8,128,128]{2,1,0:T(8,128)(2,1)S(1)} %project.1), channel_id=1, replica_groups=mesh['groups'=2,'ctx'=16,'head'=4,'pair'=2] {'head','pair'}, dimensions={0} | all-to-all | bytes 524288 | tf_op jit(solution)/shard_map/all_to_all | solution.py:490
  91.1 0.2 dispatch.1
  91.3 17.4 %all_to_all.32.x_ref = bf16[16,32,128]{2,1,0:T(8,128)(2,1)S(1)} all-to-all(bf16[16,32,128]{2,1,0:T(8,128)(2,1)S(1)} %dispatch.1), channel_id=1, replica_groups=mesh['groups'=2,'ctx'=16,'head'=4,'pair'=2] {'ctx'}, dimensions={0} | all-to-all | bytes 262144 | tf_op jit(solution)/shard_map/all_to_all | solution.py:492
  108.8 0.0 copy-done.1
  108.8 4.5 %run_expert.1 = bf16[16,2,2048]{2,1,0:T(2,128)(2,1)S(1)} custom-call(bf16[16,32,128]{2,1,0:T(8,128)(2,1)S(1)} %all_to_all.32.x_ref, f32[32,128]{1,0:T(8,128)S(1)} %get-tuple-element.24.f_ref, f32[1,2048]{1,0:T(1,128)S(1)} %bitcast.13, bf16[2048,1536]{1,0:T(8,128)(2,1)} %bitcast.14, bf16[768,2048]{1,0:T(8,128)(2,1)} %bitcast.15), custom_call_target="tpu_custom_call" | custom-call | tf_op jit(solution)/shard_map/run_expert/pallas_call | solution.py:400
  113.3 17.5 %all_to_all.33.x_ref = bf16[16,2,2048]{2,1,0:T(2,128)(2,1)S(1)} all-to-all(bf16[16,2,2048]{2,1,0:T(2,128)(2,1)S(1)} %run_expert.1), channel_id=1, replica_groups=mesh['groups'=2,'ctx'=16,'head'=4,'pair'=2] {'ctx'}, dimensions={0} | all-to-all | bytes 262144 | tf_op jit(solution)/shard_map/all_to_all | solution.py:494
  130.8 0.0 copy-done
  130.8 0.9 sum_rows.1
  131.7 11.7 %all_to_all.34.x_ref = f32[8,2,2048]{2,1,0:T(2,128)S(1)} all-to-all(f32[8,2,2048]{2,1,0:T(2,128)S(1)} %sum_rows.1), channel_id=1, replica_groups=mesh['groups'=2,'ctx'=16,'head'=4,'pair'=2] {'head','pair'}, dimensions={0} | all-to-all | bytes 262144 | tf_op jit(solution)/shard_map/all_to_all | solution.py:496
  143.4 0.7 finish.1
Async XLA Ops:
  0.0 108.8 %copy-start.1 = (f32[2048]{0:T(1024)S(1)}, f32[2048]{0:T(1024)}, u32[]{:S(2)}) copy-start(f32[2048]{0:T(1024)} %param.15) | copy-start | bytes 24580
  4.5 23.7 %collective-permute-start = (bf16[16,72,128]{2,1,0:T(8,128)(2,1)S(1)}, bf16[16,72,128]{2,1,0:T(8,128)(2,1)S(1)}, u32[]{:S(2)}, u32[]{:S(2)}) collective-permute-start(bf16[16,72,128]{2,1,0:T(8,128)(2,1)S(1)} %get-tuple-element.18), channel_id=1, source_target_pairs={{0,1},{1,0},{2,3},{3,2},{4,5},{5,4},{6,7},{7,6},{8,9},{9,8},{10,11... | collective-permute-start | bytes 884744 | tf_op jit(solution)/shard_map/ppermute | solution.py:136
  49.1 25.1 %all-to-all-start.1 = ((bf16[16,64,128]{2,1,0:T(8,128)(2,1)}), bf16[16,64,128]{2,1,0:T(8,128)(2,1)S(1)}, u32[]{:S(2)}, u32[]{:S(2)}) async-start(bf16[16,64,128]{2,1,0:T(8,128)(2,1)} %combine_all.1), calls=%async_computation.1 | async-start | bytes 524288 | tf_op jit(solution)/shard_map/all_to_all | solution.py:487
  62.3 68.5 %copy-start = (s32[16,8]{0,1:T(8,128)S(1)}, s32[16,8]{0,1:T(8,128)}, u32[]{:S(2)}) copy-start(s32[16,8]{0,1:T(8,128)} %param.16) | copy-start | bytes 1540

commit v4 on v3

v4 whole, which is shorter than its diff:
```python
import functools
import math

import jax
import jax.numpy as jnp
from jax import lax
from jax.experimental import pallas as pl
from jax.experimental.pallas import tpu as pltpu
from jax.sharding import PartitionSpec as P


F32 = jnp.float32
BF16 = jnp.bfloat16
LIMIT = 16 << 20
LOG2E = math.log2(math.e)
STATS = 8


SMEM = pl.BlockSpec(memory_space=pltpu.SMEM)
VMEM = pl.BlockSpec(memory_space=pltpu.VMEM)
HBM = pl.BlockSpec(memory_space=pltpu.HBM)


def in_hbm(x):
    return pltpu.with_memory_space_constraint(x, pltpu.HBM)


def iota(shape, dim):
    return lax.broadcasted_iota(jnp.int32, shape, dim)


def dot(a, b):
    return lax.dot_general(a, b, (((1,), (0,)), ((), ())), preferred_element_type=F32)


def as_row(column, lanes):
    n = column.shape[0]
    here = iota((n, lanes), 0) == iota((n, lanes), 1)
    return jnp.sum(jnp.where(here, jnp.broadcast_to(column, (n, lanes)), 0.0), axis=0, keepdims=True)


def as_column(row, n):
    lanes = row.shape[1]
    here = iota((n, lanes), 0) == iota((n, lanes), 1)
    return jnp.sum(jnp.where(here, jnp.broadcast_to(row, (n, lanes)), 0.0), axis=1, keepdims=True)


def pieces(row):
    first = row.astype(BF16).astype(F32)
    second = (row - first).astype(BF16).astype(F32)
    third = row - first - second
    return first, second, third


def stacked(rows, lanes):
    at = iota((STATS, lanes), 0)
    out = jnp.zeros((STATS, lanes), F32)
    for i, row in enumerate(rows):
        out = jnp.where(at == i, jnp.broadcast_to(row, (STATS, lanes)), out)
    return out


def attend_tiles(q_ref, k_ref, v_ref, o_ref, score_refs, pairs_block, ready):
    blocks, _, _, width = q_ref.shape
    tile_blocks = max(1, 128 // pairs_block)
    tile = tile_blocks * pairs_block
    steps = blocks // tile_blocks
    scale = LOG2E / math.sqrt(width)

    def scores(i):
        q = q_ref[i * tile_blocks : (i + 1) * tile_blocks].reshape(tile, width)
        score_refs[i % 2][...] = lax.dot_general(
            q, k_ref[...], (((1,), (1,)), ((), ())), preferred_element_type=F32
        )

    scores(0)
    ready()
    for i in range(steps):
        if i + 1 < steps:
            scores(i + 1)
        here = score_refs[i % 2][...]
        top = jnp.max(here, axis=1, keepdims=True)
        probs = jnp.exp2((here - top) * scale)
        total = jnp.sum(probs, axis=1, keepdims=True)
        out = dot(probs.astype(BF16), v_ref[...]) / total
        level = top * scale + jnp.log(total) * LOG2E
        for b in range(tile_blocks):
            part = slice(b * pairs_block, (b + 1) * pairs_block)
            at = i * tile_blocks + b
            o_ref[at, 0:pairs_block, :] = out[part].astype(BF16)
            row = as_row(level[part], width)
            o_ref[at, pairs_block : pairs_block + STATS, :] = stacked(pieces(row), width).astype(BF16)


def attend_first(place, queries, keys, values, residual, names, weights, pairs_block):
    blocks, _, n_head, _, unit, width = queries.shape
    length = keys.shape[0]
    quarter = (blocks, n_head, unit, width)
    tile = max(1, 128 // pairs_block) * pairs_block

    def kernel(
        place_ref, q_hbm, k_hbm, v_hbm, r_hbm, n_hbm, g_hbm,
        o_ref, q2, q3, q4, k_ref, v_ref, r_ref, facts_ref,
        q1, score_a, score_b, n_ref, g_ref, sems,
    ):
        pair, parity = place_ref[1], place_ref[3]
        small = [
            pltpu.make_async_copy(a, b, sems.at[6 + i])
            for i, (a, b) in enumerate(((r_hbm, r_ref), (n_hbm, n_ref), (g_hbm, g_ref)))
        ]
        copy_k = pltpu.make_async_copy(k_hbm, k_ref, sems.at[0])
        copy_v = pltpu.make_async_copy(v_hbm, v_ref, sems.at[1])
        choices = ((q1, 1 - parity, 1 - pair), (q2, 1 - parity, pair), (q3, parity, 1 - pair), (q4, parity, pair))
        copies = [
            pltpu.make_async_copy(q_hbm.at[:, side, :, core], ref, sems.at[2 + i])
            for i, (ref, side, core) in enumerate(choices)
        ]
        for copy in small:
            copy.start()
        copies[0].start()
        copy_k.start()
        copy_v.start()
        for copy in copies[1:]:
            copy.start()
        for copy in small:
            copy.wait()
        top, rows = n_ref.shape
        spread = (iota((rows, width), 1) % rows == iota((rows, width), 0)).astype(F32).astype(BF16)
        kept = iota((top, width), 1) // rows == iota((top, width), 0)

        def in_lanes(table):
            return jnp.sum(jnp.where(kept, dot(table.astype(BF16), spread), 0.0), axis=0, keepdims=True)

        gates = g_ref[...]
        rounded = gates.astype(BF16).astype(F32)
        facts = (in_lanes(n_ref[...].astype(F32)), in_lanes(rounded), in_lanes(gates - rounded))
        facts_ref[...] = stacked(facts, width)
        copies[0].wait()
        copy_k.wait()
        attend_tiles(q1, k_ref, v_ref, o_ref, (score_a, score_b), pairs_block, copy_v.wait)
        for copy in copies[1:]:
            copy.wait()

    return pl.pallas_call(
        kernel,
        in_specs=[SMEM] + [HBM] * 6,
        out_specs=[VMEM] * 8,
        out_shape=[jax.ShapeDtypeStruct((blocks, pairs_block + STATS, width), BF16)]
        + [jax.ShapeDtypeStruct(quarter, BF16)] * 3
        + [jax.ShapeDtypeStruct(x.shape, BF16) for x in (keys, values, residual)]
        + [jax.ShapeDtypeStruct((STATS, width), F32)],
        scratch_shapes=[pltpu.VMEM(quarter, BF16)]
        + [pltpu.VMEM((tile, length), F32)] * 2
        + [pltpu.VMEM(names.shape, names.dtype), pltpu.VMEM(weights.shape, weights.dtype)]
        + [pltpu.SemaphoreType.DMA((9,))],
        compiler_params=pltpu.CompilerParams(vmem_limit_bytes=LIMIT),
        name="attend_first",
    )(place, *[in_hbm(x) for x in (queries, keys, values, residual, names, weights)])


def attend_next(queries, keys, values, pairs_block):
    blocks, _, _, width = queries.shape
    tile = max(1, 128 // pairs_block) * pairs_block

    def kernel(q_ref, k_ref, v_ref, o_ref, score_a, score_b):
        attend_tiles(q_ref, k_ref, v_ref, o_ref, (score_a, score_b), pairs_block, lambda: None)

    return pl.pallas_call(
        kernel,
        in_specs=[VMEM] * 3,
        out_shape=jax.ShapeDtypeStruct((blocks, pairs_block + STATS, width), BF16),
        scratch_shapes=[pltpu.VMEM((tile, keys.shape[0]), F32)] * 2,
        compiler_params=pltpu.CompilerParams(vmem_limit_bytes=LIMIT),
        name="attend_next",
    )(queries, keys, values)


def levels_of(ref, pairs_block):
    stats = ref[:, pairs_block : pairs_block + STATS, :].astype(F32)
    return stats[:, 0, :] + stats[:, 1, :] + stats[:, 2, :]


def merge(partials, residual, facts, place, theirs):
    count = len(partials)
    blocks, height, width = partials[0].shape
    pairs_block = height - STATS
    height_out = height + STATS * (count - 2)

    def kernel(place_ref, *refs):
        parts, (r_ref, f_ref, o_ref) = refs[:count], refs[count:]
        levels = [levels_of(ref, pairs_block) for ref in parts]
        highest = functools.reduce(jnp.maximum, levels)
        shares = [jnp.exp2(level - highest) for level in levels]
        total = functools.reduce(jnp.add, shares)
        shares = [share / total for share in shares]
        first, second, third = pieces(highest + jnp.log(total) * LOG2E)
        for b in range(blocks):
            merged = jnp.zeros((pairs_block, width), F32)
            for ref, share in zip(parts, shares):
                merged = merged + ref[b, 0:pairs_block, :].astype(F32) * as_column(share[b : b + 1], pairs_block)
            o_ref[b, 0:pairs_block, :] = merged.astype(BF16)
        residual_all = r_ref[...].astype(F32)
        facts = tuple(f_ref[i : i + 1, :] for i in range(3))
        side = 1 - place_ref[3] if theirs else place_ref[3]
        for b in range(blocks):
            even = residual_all[:, 2 * b * width : (2 * b + 1) * width]
            odd = residual_all[:, (2 * b + 1) * width : (2 * b + 2) * width]
            own = jnp.where(jnp.broadcast_to(side, even.shape) == 0, even, odd)
            rows_b = (first[b : b + 1], second[b : b + 1], third[b : b + 1], own[0:1], own[1:2])
            o_ref[b, pairs_block:height, :] = stacked(rows_b + facts, width).astype(BF16)
            for ref in parts[2:]:
                o_ref[b, height:height_out, :] = ref[b, pairs_block:height, :]

    return pl.pallas_call(
        kernel,
        in_specs=[SMEM] + [VMEM] * (count + 2),
        out_shape=jax.ShapeDtypeStruct((blocks, height_out, width), BF16),
        compiler_params=pltpu.CompilerParams(vmem_limit_bytes=LIMIT),
        name="merge",
    )(place, *partials, residual, facts)


def combine_all(parts, rows_half, heads, peers):
    sources, height, width = parts.shape
    pairs_block = height - 2 * STATS

    def kernel(x_ref, o_hbm, acc_ref, att_ref, sem):
        level = levels_of(x_ref, pairs_block)
        share = jnp.exp2(level - jnp.max(level, axis=0, keepdims=True))
        share = share / jnp.sum(share, axis=0, keepdims=True)
        acc = jnp.zeros((pairs_block, width), F32)
        for s in range(sources):
            acc = acc + x_ref[s, 0:pairs_block, :].astype(F32) * as_column(share[s : s + 1], pairs_block)
        acc_ref[...] = acc
        by_head = [acc_ref[pl.ds(h, rows_half, stride=heads), :] for h in range(heads)]
        att_ref[...] = jnp.concatenate(by_head, axis=0).astype(BF16)
        copies = [pltpu.make_async_copy(att_ref, o_hbm.at[s], sem.at[s]) for s in range(peers)]
        for copy in copies:
            copy.start()
        for copy in copies:
            copy.wait()

    return pl.pallas_call(
        kernel,
        in_specs=[VMEM],
        out_specs=HBM,
        out_shape=pltpu.HBM((peers, pairs_block, width), BF16),
        scratch_shapes=[
            pltpu.VMEM((pairs_block, width), F32),
            pltpu.VMEM((pairs_block, width), BF16),
            pltpu.SemaphoreType.DMA((peers,)),
        ],
        compiler_params=pltpu.CompilerParams(vmem_limit_bytes=LIMIT),
        name="combine_all",
    )(parts)


def project(attended, weight, parts, place, rows_half, heads, copies):
    blocks, pairs_block, width = attended.shape
    columns = weight.shape[1]
    rows = blocks * rows_half

    def kernel(place_ref, a_ref, w_ref, s_ref, o_ref):
        a = a_ref[...].astype(F32)
        by_head = [a[:, h * rows_half : (h + 1) * rows_half, :].reshape(rows, width) for h in range(heads)]
        out = dot(jnp.concatenate(by_head, axis=1).astype(BF16), w_ref[...])
        stats_all = s_ref[:, pairs_block : pairs_block + 2 * STATS, :].astype(F32)
        same, other = stats_all[:, :STATS], stats_all[:, STATS:]
        at = iota((rows_half, columns), 0)
        first = 2 * place_ref[0]
        crossed = jnp.broadcast_to(place_ref[3], (STATS, columns)).astype(F32)
        finished = []
        for block in range(blocks):
            one, two = same[block // 2], other[block // 2]
            share = 1.0 - crossed if block % 2 == 0 else crossed
            stats = one * share + two * (1.0 - share)
            added = jnp.where(at == first, stats[3:4], 0.0) + jnp.where(at == first + 1, stats[4:5], 0.0)
            finished.append(out[block * rows_half : (block + 1) * rows_half] + added)
        out = jnp.concatenate(finished, axis=0).astype(BF16)
        for i in range(copies):
            o_ref[i] = out

    return pl.pallas_call(
        kernel,
        in_specs=[SMEM, VMEM, VMEM, VMEM],
        out_shape=jax.ShapeDtypeStruct((copies, rows, columns), BF16),
        compiler_params=pltpu.CompilerParams(vmem_limit_bytes=LIMIT),
        name="project",
    )(place, attended, weight, parts)


def selection(parts, place, sizes, fetched):
    n_ctx, n_head, n_pair, rows_own, _, capacity = sizes
    block_rows = n_head * n_pair * rows_own
    rows_all = n_ctx * block_rows
    blocks, height, width = parts.shape
    per_peer = n_ctx * capacity

    def natural(lane):
        pair = lane // (rows_all // n_pair)
        rest = lane % (rows_all // n_pair)
        block = rest // (n_head * rows_own)
        head = (rest // rows_own) % n_head
        return block, (head * n_pair + pair) * rows_own + rest % rows_own

    count_fetched = len(fetched)

    def kernel(place_ref, s_ref, *refs):
        sources, d_ref, o_ref = refs[:count_fetched], refs[count_fetched], refs[count_fetched + 1]
        targets, sems = refs[count_fetched + 2 : -1], refs[-1]
        fetches = [
            pltpu.make_async_copy(a.at[:, pl.ds(0, b.shape[1])], b, sems.at[i])
            for i, (a, b) in enumerate(zip(sources, targets))
        ]
        for fetch in fetches:
            fetch.start()
        stats = s_ref[:, height - 2 * STATS : height, :].astype(F32)
        came = iota((n_ctx, n_ctx), 1)
        came = came % blocks * 2 + jnp.where(came < blocks, place_ref[3], 1 - place_ref[3])
        order = (came == iota((n_ctx, n_ctx), 0)).astype(F32).astype(BF16)

        def in_order(row):
            rows = jnp.concatenate([stats[:, row, :], stats[:, row + STATS, :]], axis=0)
            return dot(order, rows.astype(BF16))

        listed = in_order(5)
        count = n_ctx * n_ctx
        repeated = jnp.concatenate([listed] * n_ctx, axis=0)
        expert = (iota((count, width), 0) // n_ctx * n_head * n_pair + place_ref[0] * n_pair + place_ref[1]).astype(F32)
        equal = (repeated == expert).astype(F32).astype(BF16)
        fold = (iota((width, block_rows), 0) % block_rows == iota((width, block_rows), 1)).astype(F32).astype(BF16)
        hits = dot(equal, fold)
        earlier = (iota((block_rows, block_rows), 0) < iota((block_rows, block_rows), 1)).astype(F32).astype(BF16)
        rank = dot(hits.astype(BF16), earlier)
        slot = jnp.where(hits > 0.5, rank + 1.0, 0.0).astype(BF16)
        expand = iota((count * capacity, count), 0) // capacity == iota((count * capacity, count), 1)
        slot = dot(expand.astype(F32).astype(BF16), slot).astype(BF16)
        block, row = natural(iota((block_rows, rows_all), 1))
        spread = (iota((block_rows, rows_all), 0) == row).astype(F32).astype(BF16)
        slot = dot(slot, spread)
        at = iota((count * capacity, rows_all), 0)
        block, row = natural(iota((count * capacity, rows_all), 1))
        mine = (block == (at // capacity) % n_ctx) & (slot == (at % capacity + 1).astype(F32))
        d_ref[...] = mine.astype(F32).astype(BF16)
        own = (place_ref[2] * n_head * n_pair + place_ref[0] * n_pair + place_ref[1]).astype(F32)
        same = (listed == own).astype(F32).astype(BF16)
        rank = dot(dot(same, fold).astype(BF16), earlier).astype(BF16)
        back = (iota((block_rows, width), 1) % block_rows == iota((block_rows, width), 0)).astype(F32).astype(BF16)
        twice = iota((per_peer, n_ctx), 0) // capacity == iota((per_peer, n_ctx), 1)
        twice = twice.astype(F32).astype(BF16)
        rank = dot(twice, dot(rank, back).astype(BF16))
        used = (dot(twice, same) > 0.5) & (rank == (iota((per_peer, width), 0) % capacity).astype(F32))
        gates = dot(twice, in_order(6).astype(BF16)) + dot(twice, in_order(7).astype(BF16))
        gate = jnp.sum(jnp.where(used, gates, 0.0), axis=1, keepdims=True)
        is_first = used & (iota((per_peer, width), 1) < block_rows)
        is_first = jnp.sum(jnp.where(is_first, 1.0, 0.0), axis=1, keepdims=True)
        o_ref[...] = jnp.where(iota((per_peer, width), 1) == 0, gate, is_first)
        for fetch in fetches:
            fetch.wait()

    return pl.pallas_call(
        kernel,
        in_specs=[SMEM, VMEM] + [HBM] * count_fetched,
        out_specs=[VMEM] * (2 + count_fetched),
        out_shape=[
            jax.ShapeDtypeStruct((n_ctx * per_peer, rows_all), BF16),
            jax.ShapeDtypeStruct((per_peer, width), F32),
        ]
        + [jax.ShapeDtypeStruct((x.shape[0], columns), x.dtype) for x, columns in fetched],
        scratch_shapes=[pltpu.SemaphoreType.DMA((count_fetched,))],
        compiler_params=pltpu.CompilerParams(vmem_limit_bytes=LIMIT),
        name="selection",
    )(place, parts, *[in_hbm(x) for x, columns in fetched])


def dispatch(partials, picks, n_ctx, n_head, n_pair):
    _, _, columns = partials.shape
    per_peer = picks.shape[0] // n_ctx

    def kernel(x_ref, d_ref, o_ref):
        halves = []
        for p in range(n_pair):
            acc = x_ref[p].astype(F32)
            for h in range(1, n_head):
                acc = acc + x_ref[h * n_pair + p].astype(F32)
            halves.append(acc)
        hidden = jnp.concatenate(halves, axis=0).astype(BF16)
        o_ref[...] = dot(d_ref[...], hidden).reshape(n_ctx, per_peer, columns).astype(BF16)

    return pl.pallas_call(
        kernel,
        out_shape=jax.ShapeDtypeStruct((n_ctx, per_peer, columns), BF16),
        compiler_params=pltpu.CompilerParams(vmem_limit_bytes=LIMIT),
        name="dispatch",
    )(partials, picks)


def chunk_of(units):
    return 256 if units % 256 == 0 else units


def run_expert(parts, slot_facts, gain, early, gate_up, down):
    sources, slots, columns = parts.shape
    capacity = slots // sources
    width = sources * columns
    units = down.shape[0]
    chunk = chunk_of(units)
    count = units // chunk
    starts = [units]
    for i in range(1, count):
        starts += [i * chunk, units + i * chunk]

    def kernel(x_ref, f_ref, g_ref, early_ref, up_hbm, down_hbm, y_ref, up_ref, down_ref, sems):
        ups = [
            pltpu.make_async_copy(up_hbm.at[:, pl.ds(start, chunk)], up_ref.at[i], sems.at[i])
            for i, start in enumerate(starts)
        ]
        downs = [
            pltpu.make_async_copy(
                down_hbm.at[pl.ds(i * chunk, chunk)], down_ref.at[pl.ds(i * chunk, chunk)], sems.at[len(starts) + i]
            )
            for i in range(count)
        ]
        for copy in ups + downs:
            copy.start()
        rows = jnp.concatenate([x_ref[s].astype(F32) for s in range(sources)], axis=1)
        mean = jnp.sum(rows * rows, axis=1, keepdims=True) * (1.0 / width)
        normed = (rows * lax.rsqrt(mean + 1e-06) * g_ref[...]).astype(BF16)
        inner = []
        for i in range(count):
            if i == 0:
                gate = dot(normed, early_ref[...])
            else:
                ups[2 * i - 1].wait()
                gate = dot(normed, up_ref[2 * i - 1])
            ups[2 * i].wait()
            inner.append((gate / (1.0 + jnp.exp(-gate)) * dot(normed, up_ref[2 * i])).astype(BF16))
        out = jnp.zeros((slots, width), F32)
        for i in range(count):
            downs[i].wait()
            out = out + dot(inner[i], down_ref[i * chunk : (i + 1) * chunk, :])
        out = out * f_ref[:, 0:1] + rows * f_ref[:, 1:2]
        y_ref[...] = out.astype(BF16).reshape(sources, capacity, width)

    return pl.pallas_call(
        kernel,
        in_specs=[VMEM, VMEM, VMEM, VMEM, HBM, HBM],
        out_shape=jax.ShapeDtypeStruct((sources, capacity, width), BF16),
        scratch_shapes=[
            pltpu.VMEM((len(starts), width, chunk), BF16),
            pltpu.VMEM(down.shape, BF16),
            pltpu.SemaphoreType.DMA((len(starts) + count,)),
        ],
        compiler_params=pltpu.CompilerParams(vmem_limit_bytes=24 << 20),
        name="run_expert",
    )(parts, slot_facts, gain.reshape(1, width), early, in_hbm(gate_up), in_hbm(down))


def sum_rows(returned, lists, place, sizes):
    n_ctx, n_head, n_pair, rows_own, top, capacity = sizes
    slots, width = n_ctx * capacity, returned.shape[2]
    rows = lists.shape[1]

    def kernel(place_ref, x_ref, l_ref, o_ref):
        slot = iota((slots, rows), 0)
        expert = slot // capacity * n_head * n_pair + place_ref[0] * n_pair + place_ref[1]
        hits = jnp.zeros((slots, rows), F32)
        for k in range(top):
            hits = jnp.where(l_ref[k : k + 1, :] == expert, 1.0, hits)
        earlier = (iota((rows, rows), 0) < iota((rows, rows), 1)).astype(F32).astype(BF16)
        rank = dot(hits.astype(BF16), earlier)
        taken = jnp.where(rank == (slot % capacity).astype(F32), hits, 0.0).astype(BF16)
        x = x_ref[...].reshape(slots, width)
        out = lax.dot_general(taken, x, (((0,), (0,)), ((), ())), preferred_element_type=F32)
        o_ref[...] = out.reshape(n_head * n_pair, rows_own, width)

    return pl.pallas_call(
        kernel,
        in_specs=[SMEM, VMEM, VMEM],
        out_shape=jax.ShapeDtypeStruct((n_head * n_pair, rows_own, width), F32),
        compiler_params=pltpu.CompilerParams(vmem_limit_bytes=LIMIT),
        name="sum_rows",
    )(place, returned, lists)


def finish(shares):
    def kernel(x_ref, o_ref):
        o_ref[...] = jnp.sum(x_ref[...], axis=0).astype(BF16)

    return pl.pallas_call(
        kernel,
        out_shape=jax.ShapeDtypeStruct(shares.shape[1:], BF16),
        compiler_params=pltpu.CompilerParams(vmem_limit_bytes=LIMIT),
        name="finish",
    )(shares)


def body(
    queries,
    prompt_keys,
    prompt_values,
    residual,
    out_weight,
    norm_gain,
    expert_lists,
    gate_weights,
    gate_up,
    down_proj,
):
    n_ctx = lax.axis_size("ctx")
    n_head = lax.axis_size("head")
    n_pair = lax.axis_size("pair")
    rows_own, _ = residual.shape
    _, heads, head_size = queries.shape
    _, top = expert_lists.shape
    capacity = 2
    rows_half = n_head * rows_own
    pairs_block = rows_half * heads
    sizes = (n_ctx, n_head, n_pair, rows_own, top, capacity)
    head, pair = lax.axis_index("head"), lax.axis_index("pair")
    ctx = lax.axis_index("ctx")
    place = jnp.stack([head, pair, ctx, ctx % 2]).astype(jnp.int32)

    quarters = queries.reshape(n_ctx // 2, 2, n_head, n_pair, rows_own * heads, head_size)
    keys = prompt_keys.reshape(-1, head_size)
    values = prompt_values.reshape(-1, head_size)
    lists, weights = expert_lists.T, gate_weights.T
    cores = [(i, i ^ 1) for i in range(n_pair)]
    chips = [(i, i ^ 1) for i in range(n_ctx)]
    parities = [list(range(i, n_ctx, 2)) for i in range(2)]
    away, q_two, q_three, q_four, keys, values, residual, facts = attend_first(
        place, quarters, keys, values, residual, lists, weights, pairs_block
    )
    swapped = lax.ppermute(away, "pair", cores)
    here = attend_next(q_two, keys, values, pairs_block)
    passed = merge((here, swapped), residual, facts, place, True)
    passed, q_three, q_four = lax.optimization_barrier((passed, q_three, q_four))
    from_chip = lax.ppermute(passed, "ctx", chips)
    away = attend_next(q_three, keys, values, pairs_block)
    away, q_four = lax.optimization_barrier((away, q_four))
    swapped = lax.ppermute(away, "pair", cores)
    here = attend_next(q_four, keys, values, pairs_block)
    merged = merge((here, swapped, from_chip), residual, facts, place, False)
    parts = lax.all_to_all(merged, "ctx", 0, 0, axis_index_groups=parities, tiled=True)
    copies = combine_all(parts, rows_half, heads, n_ctx)
    gate_up_here = gate_up[0]
    early = chunk_of(down_proj.shape[1])
    picks, slot_facts, weight_here, early_here = selection(
        parts, place, sizes, ((out_weight, out_weight.shape[1]), (gate_up_here, early))
    )
    attended = lax.all_to_all(copies, "ctx", 0, 0, tiled=True)
    attended, picks, slot_facts = lax.optimization_barrier((attended, picks, slot_facts))
    partial = project(attended, weight_here, parts, place, rows_half, heads, n_head * n_pair)
    partials = lax.all_to_all(partial, ("head", "pair"), 0, 0, tiled=True)
    sending = dispatch(partials, picks, n_ctx, n_head, n_pair)
    arrived = lax.all_to_all(sending, "ctx", 0, 0, tiled=True)
    produced = run_expert(arrived, slot_facts, norm_gain, early_here, gate_up_here, down_proj[0])
    returned = lax.all_to_all(produced, "ctx", 0, 0, tiled=True)
    weighted = sum_rows(returned, lists, place, sizes)
    shares = lax.all_to_all(weighted, ("head", "pair"), 0, 0, tiled=True)
    return finish(shares)


def solution(mesh):
    in_specs = (
        P("groups", "head", None),
        P(("groups", "ctx", "pair"), "head", None),
        P(("groups", "ctx", "pair"), "head", None),
        P(("groups", "ctx", "head", "pair"), None),
        P("head", "ctx"),
        P(),
        P(("groups", "ctx"), None),
        P(("groups", "ctx"), None),
        P(("ctx", "head", "pair"), None, None),
        P(("ctx", "head", "pair"), None, None),
    )
    out_specs = P(("groups", "ctx", "head", "pair"), None)
    return jax.shard_map(body, mesh=mesh, in_specs=in_specs, out_specs=out_specs, check_vma=False)
```

time: 145 us -> 144 us (level)
  starting transfers between devices: 32 us -> 26 us
  waiting for transfers between devices: 11.9 us -> 13.9 us
  Pallas kernels: 18.4 us -> 20.2 us
    all_to_all x1, starting transfers between devices: 11.4 us -> 5.16 us  [body(): attended = lax.all_to_all(copies, 'ctx', 0, 0, tiled=True)]
    ppermute x1 -> x3, waiting for transfers between devices: 0.01 us -> 3.28 us  [the longest x1 3.28 us: body(): from_chip = lax.ppermute(passed, 'ctx', chips)]
    all_to_all x1, blocking collectives: 16.2 us -> 18.1 us  [body(): partials = lax.all_to_all(partial, ('head', 'pair'), 0, 0, tiled=True)]
    pallas_call x4 -> x7, Pallas kernels: 13.1 us -> 14.8 us  [the longest x3 5.17 us: attend_next(): pl.pallas_call(kernel, in_specs=[VMEM] * 3, out_shape=jax.ShapeDtypeStruc...]
    ppermute x1 -> x3, starting transfers between devices: 20.5 us -> 20.8 us  [the longest x2 20.7 us: body(): swapped = lax.ppermute(away, 'pair', cores)]
  transfers between devices with their start and end apart: 2 -> 4, of which waited for: 1 -> 2; matrix products, arithmetic and copies ran while one was open for 0% -> 0% of each run, Pallas kernels for 3% -> 4%
where the time goes in v4:
time: 144 us; the launch traced here: 143 us
  blocking collectives  82.7 us (57%)
  starting transfers between devices  26 us (18%)
  Pallas kernels  20.2 us (14%)
  waiting for transfers between devices  13.9 us (10%)
    ppermute x2, starting transfers between devices, body(): swapped = lax.ppermute(away, 'pair', cores)  20.7 us
    all_to_all x1, blocking collectives, body(): lax.all_to_all(merged, 'ctx', 0, 0, axis_index_groups=parities, tiled=True)  18.9 us
    all_to_all x1, blocking collectives, body(): partials = lax.all_to_all(partial, ('head', 'pair'), 0, 0, tiled=True)  18.1 us
    all_to_all x1, blocking collectives, body(): returned = lax.all_to_all(produced, 'ctx', 0, 0, tiled=True)  17.5 us
    all_to_all x1, blocking collectives, body(): arrived = lax.all_to_all(sending, 'ctx', 0, 0, tiled=True)  16.6 us
    all_to_all x1, blocking collectives, body(): shares = lax.all_to_all(weighted, ('head', 'pair'), 0, 0, tiled=True)  11.7 us
    all_to_all x1, waiting for transfers between devices, body(): attended = lax.all_to_all(copies, 'ctx', 0, 0, tiled=True)  10.6 us
    pallas_call x3, Pallas kernels, attend_next(): pl.pallas_call(kernel, in_specs=[VMEM] * 3, out_shape=jax.ShapeDtypeStruc...  5.17 us
  transfers between devices with their start and end apart: 4, of which 2 were waited for; matrix products, arithmetic and copies ran while one was open for 0% of the time, Pallas kernels for 4%

profile of v4, /device:TPU:33, one launch (start us, length us, event | category | flops | bytes accessed | tf_op | source)
XLA Modules:
  0.0 143.1 jit_solution(15694460817581172274)
XLA Ops:
  0.0 0.1 pad_add_fusion.place_ref
  0.1 3.7 %attend_first.1 = (bf16[8,72,128]{2,1,0:T(8,128)(2,1)S(1)}, bf16[8,4,16,128]{3,2,1,0:T(8,128)(2,1)S(1)}, bf16[8,4,16,128]{3,2,1,0:T(8,128)(2,1)S(1)}, bf16[8,4,1...) custom-call(s32[4]{0:T(128)S(1)} %pad_add_fusion.place_ref, ...), custom_call_target="tpu_custom_call" | custom-call | tf_op jit(solution)/shard_map/attend_first/pallas_call | solution.py:144
  3.8 20.5 %collective-permute-start = (bf16[8,72,128]{2,1,0:T(8,128)(2,1)S(1)}, bf16[8,72,128]{2,1,0:T(8,128)(2,1)S(1)}, u32[]{:S(2)}, u32[]{:S(2)}) collective-permute-start(bf16[8,72,128]{2,1,0:T(8,128)(2,1)S(1)} %get-tuple-element.28), channel_id=1, source_target_pairs={{0,1},{1,0},{2,3},{3,2},{4,5},{5,4},{6,7},{7,6},{8,9},{9,8},{10,11... | collective-permute-start | bytes 442376 | tf_op jit(solution)/shard_map/ppermute | solution.py:534
  24.3 1.7 %attend_next.3.refs_0_ = bf16[8,72,128]{2,1,0:T(8,128)(2,1)S(1)} custom-call(bf16[8,4,16,128]{3,2,1,0:T(8,128)(2,1)S(1)} %get-tuple-element.25.q_ref, bf16[2048,128]{1,0:T(8,128)(2,1)S(1)} %get-tuple-element.26.k_ref, bf16[2048,128]{1,0:T(8,128)(2,1)S(1)} %get-tuple-element.27.v_ref), custom_call_target="tpu_custom_call" | custom-call | tf_op jit(solution)/shard_map/attend_next/pallas_call | solution.py:168
  26.1 0.0 collective-permute-done.refs_1_
  26.1 0.8 merge.2
  26.8 1.7 %attend_next.4 = bf16[8,72,128]{2,1,0:T(8,128)(2,1)S(1)} custom-call(bf16[8,4,16,128]{3,2,1,0:T(8,128)(2,1)S(1)} %get-tuple-element.33.q_ref, bf16[2048,128]{1,0:T(8,128)(2,1)S(1)} %get-tuple-element.26.k_ref, bf16[2048,128]{1,0:T(8,128)(2,1)S(1)} %get-tuple-element.27.v_ref), custom_call_target="tpu_custom_call" | custom-call | tf_op jit(solution)/shard_map/attend_next/pallas_call | solution.py:168
  28.6 0.0 copy-start.1
  28.6 0.2 collective-permute-start.1
  28.7 0.1 collective-permute-start.2
  28.9 1.7 %attend_next.5.refs_0_ = bf16[8,72,128]{2,1,0:T(8,128)(2,1)S(1)} custom-call(bf16[8,4,16,128]{3,2,1,0:T(8,128)(2,1)S(1)} %get-tuple-element.35.q_ref, bf16[2048,128]{1,0:T(8,128)(2,1)S(1)} %get-tuple-element.26.k_ref, bf16[2048,128]{1,0:T(8,128)(2,1)S(1)} %get-tuple-element.27.v_ref), custom_call_target="tpu_custom_call" | custom-call | tf_op jit(solution)/shard_map/attend_next/pallas_call | solution.py:168
  30.6 0.0 collective-permute-done.1.refs_1_
  30.6 3.3 %collective-permute-done.2.refs_2_ = bf16[8,72,128]{2,1,0:T(8,128)(2,1)S(1)} collective-permute-done((bf16[8,72,128]{2,1,0:T(8,128)(2,1)S(1)}, bf16[8,72,128]{2,1,0:T(8,128)(2,1)S(1)}, u32[]{:S(2)}, u32[]{:S(2)}) %collective-permute-start.2) | collective-permute-done | bytes 147488 | tf_op jit(solution)/shard_map/ppermute | solution.py:538
  33.9 0.8 merge.3
  34.7 18.9 %all_to_all.30.x_ref.s_ref = bf16[8,80,128]{2,1,0:T(8,128)(2,1)S(1)} all-to-all(bf16[8,80,128]{2,1,0:T(8,128)(2,1)S(1)} %merge.3), channel_id=1, replica_groups={{0,16,32,48,64,80,96,112},{8,24,40,56,72,88,104,120},{1,17,33,49,65,81,..., dimensions={0} | all-to-all | bytes 327680 | tf_op jit(solution)/shard_map/all_to_all | solution.py:544
  53.6 1.0 combine_all.1
  54.7 5.2 %all-to-all-start.1 = ((bf16[16,64,128]{2,1,0:T(8,128)(2,1)}), bf16[16,64,128]{2,1,0:T(8,128)(2,1)S(1)}, u32[]{:S(2)}, u32[]{:S(2)}) async-start(bf16[16,64,128]{2,1,0:T(8,128)(2,1)} %combine_all.1), calls=%async_computation.1 | async-start | bytes 524288 | tf_op jit(solution)/shard_map/all_to_all | solution.py:551
  59.8 1.9 %selection.1 = (bf16[512,256]{1,0:T(8,128)(2,1)S(1)}, f32[32,128]{1,0:T(8,128)S(1)}, bf16[1024,128]{1,0:T(8,128)(2,1)S(1)}, bf16[2048,256]{1,0:T(8,128)(2,1)S(1)}) custom-call(s32[4]{0:T(128)S(1)} %pad_add_fusion.place_ref, bf16[8,80,128]{2,1,0:T(8,128)(2,1)S(1)} %all_to_all.30.x_ref.s_ref, bf16[1024,128]{1,0:T(8,128)(2,1)} %refs_0_.1, ...), custom_call_target="tpu_custom_call" | custom-call | tf_op jit(solution)/shard_map/selection/pallas_call | solution.py:361
  61.7 10.6 %all-to-all-done.1.a_ref = bf16[16,64,128]{2,1,0:T(8,128)(2,1)S(1)} async-done(((bf16[16,64,128]{2,1,0:T(8,128)(2,1)}), bf16[16,64,128]{2,1,0:T(8,128)(2,1)S(1)}, u32[]{:S(2)}, u32[]{:S(2)}) %all-to-all-start.1) | async-done | bytes 262176 | tf_op jit(solution)/shard_map/all_to_all | solution.py:551
  72.3 0.8 project.1
  73.1 0.0 copy-start
  73.1 18.1 %all_to_all.31.x_ref = bf16[8,128,128]{2,1,0:T(8,128)(2,1)S(1)} all-to-all(bf16[8,128,128]{2,1,0:T(8,128)(2,1)S(1)} %project.1), channel_id=1, replica_groups=mesh['groups'=2,'ctx'=16,'head'=4,'pair'=2] {'head','pair'}, dimensions={0} | all-to-all | bytes 524288 | tf_op jit(solution)/shard_map/all_to_all | solution.py:554
  91.2 0.2 dispatch.1
  91.4 16.6 %all_to_all.32.x_ref = bf16[16,32,128]{2,1,0:T(8,128)(2,1)S(1)} all-to-all(bf16[16,32,128]{2,1,0:T(8,128)(2,1)S(1)} %dispatch.1), channel_id=1, replica_groups=mesh['groups'=2,'ctx'=16,'head'=4,'pair'=2] {'ctx'}, dimensions={0} | all-to-all | bytes 262144 | tf_op jit(solution)/shard_map/all_to_all | solution.py:556
  108.0 0.0 copy-done.1
  108.0 4.3 %run_expert.1 = bf16[16,2,2048]{2,1,0:T(2,128)(2,1)S(1)} custom-call(bf16[16,32,128]{2,1,0:T(8,128)(2,1)S(1)} %all_to_all.32.x_ref, f32[32,128]{1,0:T(8,128)S(1)} %get-tuple-element.43.f_ref, f32[1,2048]{1,0:T(1,128)S(1)} %bitcast.14, bf16[2048,256]{1,0:T(8,128)(2,1)S(1)} %get-tuple-element.44.early_ref, bf16[2048,1536]{1,0:T(8,128)(2,1)} %bitcast.16, ...), custom_call_target="tpu_custom_call" | custom-call | tf_op jit(solution)/shard_map/run_expert/pallas_call | solution.py:445
  112.4 17.5 %all_to_all.33.x_ref = bf16[16,2,2048]{2,1,0:T(2,128)(2,1)S(1)} all-to-all(bf16[16,2,2048]{2,1,0:T(2,128)(2,1)S(1)} %run_expert.1), channel_id=1, replica_groups=mesh['groups'=2,'ctx'=16,'head'=4,'pair'=2] {'ctx'}, dimensions={0} | all-to-all | bytes 262144 | tf_op jit(solution)/shard_map/all_to_all | solution.py:558
  129.8 0.0 copy-done
  129.8 0.9 sum_rows.1
  130.7 11.7 %all_to_all.34.x_ref = f32[8,2,2048]{2,1,0:T(2,128)S(1)} all-to-all(f32[8,2,2048]{2,1,0:T(2,128)S(1)} %sum_rows.1), channel_id=1, replica_groups=mesh['groups'=2,'ctx'=16,'head'=4,'pair'=2] {'head','pair'}, dimensions={0} | all-to-all | bytes 262144 | tf_op jit(solution)/shard_map/all_to_all | solution.py:560
  142.4 0.7 finish.1
Async XLA Ops:
  3.8 22.3 %collective-permute-start = (bf16[8,72,128]{2,1,0:T(8,128)(2,1)S(1)}, bf16[8,72,128]{2,1,0:T(8,128)(2,1)S(1)}, u32[]{:S(2)}, u32[]{:S(2)}) collective-permute-start(bf16[8,72,128]{2,1,0:T(8,128)(2,1)S(1)} %get-tuple-element.28), channel_id=1, source_target_pairs={{0,1},{1,0},{2,3},{3,2},{4,5},{5,4},{6,7},{7,6},{8,9},{9,8},{10,11... | collective-permute-start | bytes 442376 | tf_op jit(solution)/shard_map/ppermute | solution.py:534
  28.6 79.5 %copy-start.1 = (f32[2048]{0:T(1024)S(1)}, f32[2048]{0:T(1024)}, u32[]{:S(2)}) copy-start(f32[2048]{0:T(1024)} %param.15) | copy-start | bytes 24580
  28.6 2.0 %collective-permute-start.1 = (bf16[8,72,128]{2,1,0:T(8,128)(2,1)S(1)}, bf16[8,72,128]{2,1,0:T(8,128)(2,1)S(1)}, u32[]{:S(2)}, u32[]{:S(2)}) collective-permute-start(bf16[8,72,128]{2,1,0:T(8,128)(2,1)S(1)} %attend_next.4), channel_id=1, source_target_pairs={{0,1},{1,0},{2,3},{3,2},{4,5},{5,4},{6,7},{7,6},{8,9},{9,8},{10,11... | collective-permute-start | bytes 442376 | tf_op jit(solution)/shard_map/ppermute | solution.py:541
  28.7 5.2 %collective-permute-start.2 = (bf16[8,72,128]{2,1,0:T(8,128)(2,1)S(1)}, bf16[8,72,128]{2,1,0:T(8,128)(2,1)S(1)}, u32[]{:S(2)}, u32[]{:S(2)}) collective-permute-start(bf16[8,72,128]{2,1,0:T(8,128)(2,1)S(1)} %merge.2), channel_id=1, source_target_pairs={{0,8},{8,0},{16,24},{24,16},{32,40},{40,32},{48,56},{56,48},{64,72... | collective-permute-start | bytes 442376 | tf_op jit(solution)/shard_map/ppermute | solution.py:538
  54.7 17.7 %all-to-all-start.1 = ((bf16[16,64,128]{2,1,0:T(8,128)(2,1)}), bf16[16,64,128]{2,1,0:T(8,128)(2,1)S(1)}, u32[]{:S(2)}, u32[]{:S(2)}) async-start(bf16[16,64,128]{2,1,0:T(8,128)(2,1)} %combine_all.1), calls=%async_computation.1 | async-start | bytes 524288 | tf_op jit(solution)/shard_map/all_to_all | solution.py:551
  73.1 56.7 %copy-start = (s32[16,8]{0,1:T(8,128)S(1)}, s32[16,8]{0,1:T(8,128)}, u32[]{:S(2)}) copy-start(s32[16,8]{0,1:T(8,128)} %param.16) | copy-start | bytes 1540
